TPU v7x, 64 devices: a 2x2x8 block of a 4x4x8 slice. The times are simulated.
64 devices in a mesh: rep: 4 (over x, y), dp: 16 (over z, core).
Axes of the slice: x: 2, y: 2, z: 8, core: 2. Of those that a mesh axis runs over, the one named last changes fastest.
The devices are a block of a 4x4x8 slice.
Arguments:
- x: bfloat16 [64, 1024, 768], P(('rep', 'dp')), parts along dimension 0
- dy: bfloat16 [64, 1024, 768], P(('rep', 'dp')), parts along dimension 0
- w_gate: bfloat16 [2, 768, 3072], replicated
- w_up: bfloat16 [2, 768, 3072], replicated
- w_down: bfloat16 [2, 3072, 768], replicated
- m_w_gate: float32 [2, 768, 3072], P(None, 'dp')
- m_w_up: float32 [2, 768, 3072], P(None, 'dp')
- m_w_down: float32 [2, 3072, 768], P(None, 'dp')
- v_w_gate: float32 [2, 768, 3072], P(None, 'dp')
- v_w_up: float32 [2, 768, 3072], P(None, 'dp')
- v_w_down: float32 [2, 3072, 768], P(None, 'dp')
Outputs:
- output 1: bfloat16 [8, 768, 3072], P('rep'), parts along dimension 0
- output 2: bfloat16 [8, 768, 3072], P('rep'), parts along dimension 0
- output 3: bfloat16 [8, 3072, 768], P('rep'), parts along dimension 0
- output 4: float32 [8, 768, 3072], P('rep', 'dp'), parts along dimension 0
- output 5: float32 [8, 768, 3072], P('rep', 'dp'), parts along dimension 0
- output 6: float32 [8, 3072, 768], P('rep', 'dp'), parts along dimension 0
- output 7: float32 [8, 768, 3072], P('rep', 'dp'), parts along dimension 0
- output 8: float32 [8, 768, 3072], P('rep', 'dp'), parts along dimension 0
- output 9: float32 [8, 3072, 768], P('rep', 'dp'), parts along dimension 0
There are 4 independent parts. A program takes and returns all parts, laid end to end along the dimension named above; an argument that names none is the same for every part.
All inputs are finite; a program needn't handle non-finite values.
Results may differ from a plain program's by a relative error of at most 0.022.
Values are sent between devices in bfloat16 or wider.
A program may use at most 768 MiB of HBM per device.

v0:
```python
import jax
import jax.numpy as jnp
from jax import lax

NAMES = ("w_gate", "w_up", "w_down")


def matmul(a, w):
    return jnp.dot(a, w, preferred_element_type=jnp.float32).astype(jnp.bfloat16)


def normed(h):
    wide = h.astype(jnp.float32)
    scale = lax.rsqrt(jnp.mean(wide**2, -1, keepdims=True) + 1e-6)
    return (wide * scale).astype(jnp.bfloat16)


def layer(h, w):
    a = normed(h)
    gate = jnp.dot(a, w["w_gate"], preferred_element_type=jnp.float32)
    up = jnp.dot(a, w["w_up"], preferred_element_type=jnp.float32)
    return h + matmul((jax.nn.silu(gate) * up).astype(jnp.bfloat16), w["w_down"])


def adamw(w, m, v, g):
    m = 0.9 * m + 0.1 * g
    v = 0.95 * v + 0.05 * g * g
    step = m * lax.rsqrt(v + 1e-8) + 0.1 * w
    return (w - 0.02 * step).astype(jnp.bfloat16), m, v


def clipped(gradients, sum_of_squares, count):
    factor = jnp.minimum(1.0, 0.5 * lax.rsqrt(sum_of_squares / count + 1e-30))
    return [g * factor for g in gradients]


def stack(weights, h):
    for number in range(weights["w_gate"].shape[0]):
        h = layer(h, {name: w[number] for name, w in weights.items()})
    return h


def solution(mesh):
    groups = mesh.shape["rep"]

    def step(x, dy, *arrays):
        weights, m, v = (arrays[i : i + 3] for i in (0, 3, 6))
        x, dy = (t.reshape(groups, -1, *t.shape[1:]) for t in (x, dy))

        def of_a_group(x, dy):
            _, back = jax.vjp(lambda w: stack(w, x), dict(zip(NAMES, weights, strict=True)))
            by_weights = back(dy)[0]
            gradients = [by_weights[name].astype(jnp.float32) for name in NAMES]
            gradients = clipped(gradients, sum(jnp.sum(g * g) for g in gradients), sum(g.size for g in gradients))
            new = [adamw(w.astype(jnp.float32), m, v, g) for w, m, v, g in zip(weights, m, v, gradients, strict=True)]
            return tuple(one[which] for which in range(3) for one in new)

        return tuple(t.reshape(-1, *t.shape[2:]) for t in jax.vmap(of_a_group)(x, dy))

    return step
```

profile of v0, /device:TPU:21, one launch (start us, length us, event | category | flops | bytes accessed | tf_op | source)
XLA Modules:
  0.0 755.3 jit_solution(5211783422719267041)
XLA Ops:
  18.8 8.8 %fusion.58 = f32[1024,3072]{1,0:T(8,128)S(1)} fusion(bf16[2,768,3072]{2,1,0:T(8,128)(2,1)} %param.3, bf16[1,1024,768]{2,1,0:T(8,128)(2,1)S(1)} %copy-done.6, f32[1024]{0:T(1024)S(1)} %add_rsqrt_fusion), kind=kOutput, calls=%fused_computation.66 | convolution fusion | flops 4834197504 | bytes 18878464 | tf_op jit(solution)/vmap(jvp())/dot_general | solution.py:21
  32.2 10.4 %fusion.75 = (f32[1024]{0:T(1024)S(1)}, bf16[1,1,1024,768]{2,3,1,0:T(8,128)(2,1)S(1)}) fusion(bf16[1024,3072]{1,0:T(8,128)(2,1)S(1)} %fusion.26, bf16[2,3072,768]{2,1,0:T(8,128)(2,1)} %param.4, bf16[1,1024,768]{1,2,0:T(8,128)(2,1)} %copy), kind=kOutput, calls=%fused_computation.86 | convolution fusion | flops 4835769344 | bytes 14159872 | tf_op jit(solution)/vmap(jvp())/dot_general | solution.py:9
  50.3 22.7 %fusion.52 = f32[1024,3072]{1,0:T(8,128)} fusion(bf16[2,768,3072]{2,1,0:T(8,128)(2,1)} %param.3, bf16[1,1,1024,768]{2,3,1,0:T(8,128)(2,1)S(1)} %get-tuple-element.10, f32[1024]{0:T(1024)S(1)} %bitcast.349), kind=kOutput, calls=%fused_computation.60 | convolution fusion | flops 4834197504 | bytes 18878464 | tf_op jit(solution)/vmap(jvp())/dot_general | solution.py:21
  72.9 11.8 %fusion.35 = f32[1,3072,768]{2,1,0:T(8,128)} fusion(f32[1024,3072]{1,0:T(8,128)} %fusion.52, f32[1024,3072]{1,0:T(8,128)S(1)} %fusion.49, bf16[1,1024,768]{2,1,0:T(8,128)(2,1)S(1)} %copy-done.9), kind=kOutput, calls=%fused_computation.43 | convolution fusion | flops 4850712576 | bytes 36175872 | tf_op jit(solution)/vmap(transpose(jvp()))/dot_general | solution.py:9
  97.0 13.6 %fusion.6 = bf16[1024,3072]{1,0:T(8,128)(2,1)} fusion(f32[1024,3072]{1,0:T(8,128)} %copy-done, f32[1024,3072]{1,0:T(8,128)} %fusion.52, bf16[1024,3072]{1,0:T(8,128)(2,1)S(1)} %convolution_convert_fusion.1), kind=kLoop, calls=%fused_computation.11 | loop fusion | flops 37748736 | bytes 37748736
  110.6 10.6 %fusion.78 = bf16[1024,768]{0,1:T(8,128)(2,1)} fusion(bf16[2,768,3072]{2,1,0:T(8,128)(2,1)} %param.3, bf16[1024,3072]{1,0:T(8,128)(2,1)} %copy-done.5, f32[1024,3072]{1,0:T(8,128)S(1)} %bitcast.344), kind=kOutput, calls=%fused_computation.93 | convolution fusion | flops 4851499008 | bytes 25165824 | tf_op jit(solution)/vmap(transpose(jvp()))/dot_general | solution.py:21
  121.2 10.1 %fusion.77 = (f32[1024]{0:T(1024)S(1)}, bf16[1024,768]{0,1:T(8,128)(2,1)S(1)}) fusion(bf16[1,1,1024,768]{2,3,1,0:T(8,128)(2,1)} %copy-done.1, bf16[1024,768]{0,1:T(8,128)(2,1)} %fusion.78, bf16[1024,3072]{1,0:T(8,128)(2,1)} %fusion.6, bf16[2,768,3072]{2,1,0:T(8,128)(2,1)} %param), kind=kOutput, calls=%fused_computation.88 | convolution fusion | flops 4835769344 | bytes 15732736 | tf_op jit(solution)/vmap(transpose(jvp()))/dot_general | solution.py:20
  133.6 10.3 %convolution_bitcast_fusion = f32[1,3072,768]{2,1,0:T(8,128)} fusion(bf16[1024,3072]{1,0:T(8,128)(2,1)} %copy-done.8, bf16[1024,768]{0,1:T(8,128)(2,1)S(1)} %fusion.92), kind=kOutput, calls=%fused_computation.46 | convolution fusion | flops 4831838208 | bytes 17301504 | tf_op jit(solution)/vmap(transpose(jvp()))/dot_general | solution.py:9
  144.0 11.4 %fusion.38 = f32[1,768,3072]{2,1,0:T(8,128)} fusion(bf16[1024,3072]{1,0:T(8,128)(2,1)} %copy-done.5, f32[1024,3072]{1,0:T(8,128)} %copy-done, bf16[1,1,1024,768]{2,3,1,0:T(8,128)(2,1)S(1)} %copy-done.2, f32[1024]{0:T(1024)S(1)} %bitcast.351), kind=kOutput, calls=%fused_computation.44 | convolution fusion | flops 4853071872 | bytes 29888512 | tf_op jit(solution)/vmap(transpose(jvp()))/dot_general | solution.py:21
  165.8 10.6 %fusion.41 = f32[1,768,3072]{2,1,0:T(8,128)} fusion(bf16[1024,3072]{1,0:T(8,128)(2,1)S(1)} %convolution_convert_fusion, f32[1024,3072]{1,0:T(8,128)} %copy-done.3, bf16[1,1024,768]{1,2,0:T(8,128)(2,1)S(1)} %copy-done.10, f32[1024]{0:T(1024)S(1)} %copy-done.15), kind=kOutput, calls=%fused_computation.45 | convolution fusion | flops 4853071872 | bytes 29888512 | tf_op jit(solution)/vmap(transpose(jvp()))/dot_general | solution.py:21
  176.5 10.4 %convolution_bitcast_fusion.1 = f32[1,768,3072]{2,1,0:T(8,128)} fusion(bf16[1024,3072]{1,0:T(8,128)(2,1)} %fusion.6, bf16[1,1,1024,768]{2,3,1,0:T(8,128)(2,1)S(1)} %copy-done.2, f32[1024]{0:T(1024)S(1)} %bitcast.352), kind=kOutput, calls=%fused_computation.48 | convolution fusion | flops 4834197504 | bytes 17305600 | tf_op jit(solution)/vmap(transpose(jvp()))/dot_general | solution.py:20
  187.1 16.0 %fusion.44 = f32[1,768,3072]{2,1,0:T(8,128)} fusion(f32[1024,3072]{1,0:T(8,128)} %copy-done.3, f32[1024,3072]{1,0:T(8,128)} %copy-done.4, bf16[1024,3072]{1,0:T(8,128)(2,1)} %copy-done.17, bf16[1,1024,768]{1,2,0:T(8,128)(2,1)S(1)} %copy-done.10, f32[1024]{0:T(1024)S(1)} %copy-done.15), kind=kOutput, calls=%fused_computation.50 | convolution fusion | flops 4868800512 | bytes 42471424 | tf_op jit(solution)/vmap(transpose(jvp()))/dot_general | solution.py:20
  206.1 21.3 %reduce-scatter.29.cloned.1.call-done = f32[1,192,768]{2,1,0:T(8,128)} async-done(((f32[1,3072,768]{2,1,0:T(8,128)}), f32[1,192,768]{2,1,0:T(8,128)}) %reduce-scatter.29.cloned.1.call-update) | async-done | bytes 589840
  229.4 68.9 %reduce-scatter.23.cloned.1.call-done = f32[1,48,3072]{2,1,0:T(8,128)} async-done(((f32[1,768,3072]{2,1,0:T(8,128)}), f32[1,48,3072]{2,1,0:T(8,128)}) %reduce-scatter.23.cloned.1.call-update) | async-done | bytes 589840
  299.5 70.3 %reduce-scatter.25.cloned.1.call-done = f32[1,48,3072]{2,1,0:T(8,128)} async-done(((f32[1,768,3072]{2,1,0:T(8,128)}), f32[1,48,3072]{2,1,0:T(8,128)}) %reduce-scatter.25.cloned.1.call-update) | async-done | bytes 589840
  371.8 69.4 %reduce-scatter.19.cloned.1.call-done = f32[1,48,3072]{2,1,0:T(8,128)} async-done(((f32[1,768,3072]{2,1,0:T(8,128)}), f32[1,48,3072]{2,1,0:T(8,128)}) %reduce-scatter.19.cloned.1.call-update) | async-done | bytes 589840
  442.2 70.3 %reduce-scatter.21.cloned.1.call-done = f32[1,48,3072]{2,1,0:T(8,128)} async-done(((f32[1,768,3072]{2,1,0:T(8,128)}), f32[1,48,3072]{2,1,0:T(8,128)}) %reduce-scatter.21.cloned.1.call-update) | async-done | bytes 589840
  516.5 27.4 %all-reduce.16 = f32[1]{0:T(128)} all-reduce(f32[1]{0:T(128)} %bitcast.50), channel_id=5, replica_groups=mesh['rep'=4,'dp'=16] {'dp'}, use_global_device_ids=true, to_apply=%region_3.4.clone | all-reduce | flops 1 | bytes 8 | tf_op jit(solution)/vmap()/reduce_sum | solution.py:54
  556.5 51.0 %all-gather.14.cloned.1.call-done = bf16[1,2,3072,768]{3,2,1,0:T(8,128)(2,1)} async-done(((bf16[1,2,192,768]{3,2,1,0:T(8,128)(2,1)}), bf16[1,2,3072,768]{3,2,1,0:T(8,128)(2,1)}) %all-gather.14.cloned.1.call-update) | async-done | bytes 9437200 | tf_op jit(solution)/reshape | solution.py:58
  607.5 58.2 %all-gather.10.cloned.1.call-done = bf16[1,2,768,3072]{3,2,1,0:T(8,128)(2,1)} async-done(((bf16[1,2,48,3072]{3,2,1,0:T(8,128)(2,1)}), bf16[1,2,768,3072]{3,2,1,0:T(8,128)(2,1)}) %all-gather.10.cloned.1.call-update) | async-done | bytes 9437200 | tf_op jit(solution)/reshape | solution.py:58
  665.7 58.2 %all-gather.12.cloned.1.call-done = bf16[1,2,768,3072]{3,2,1,0:T(8,128)(2,1)} async-done(((bf16[1,2,48,3072]{3,2,1,0:T(8,128)(2,1)}), bf16[1,2,768,3072]{3,2,1,0:T(8,128)(2,1)}) %all-gather.12.cloned.1.call-update) | async-done | bytes 9437200 | tf_op jit(solution)/reshape | solution.py:58
  723.9 8.3 %copy.5 = bf16[2,768,3072]{2,1,0:T(8,128)(2,1)} copy(bf16[2,768,3072]{2,1,0:T(8,128)(2,1)} %bitcast.346) | data formatting | bytes 18874368
  732.2 8.3 %copy.6 = bf16[2,768,3072]{2,1,0:T(8,128)(2,1)} copy(bf16[2,768,3072]{2,1,0:T(8,128)(2,1)} %bitcast.347) | data formatting | bytes 18874368
  740.6 8.0 %copy.7 = bf16[2,3072,768]{2,1,0:T(8,128)(2,1)} copy(bf16[2,3072,768]{2,1,0:T(8,128)(2,1)} %bitcast.345) | data formatting | bytes 18874368
  (88 shorter events, 71.3 us)
Async XLA Ops:
  7.2 4.6 copy-start.6
  7.2 197.8 %reduce-scatter.27.cloned.1.call-start = ((), (), s32[]{:S(2)}) async-start(), calls=%async_computation.13 | async-start | bytes 10027008
  11.8 7.0 copy-start.14
  18.8 8.8 %copy-start.3 = (f32[1024,3072]{1,0:T(8,128)}, f32[1024,3072]{1,0:T(8,128)S(1)}, u32[]{:S(2)}) copy-start(f32[1024,3072]{1,0:T(8,128)S(1)} %fusion.60) | copy-start | bytes 37748740
  32.2 10.4 %copy-start.8 = (bf16[1024,3072]{1,0:T(8,128)(2,1)}, bf16[1024,3072]{1,0:T(8,128)(2,1)S(1)}, u32[]{:S(2)}) copy-start(bf16[1024,3072]{1,0:T(8,128)(2,1)S(1)} %fusion.26) | copy-start | bytes 18874372
  42.6 7.7 %copy-start.1 = (bf16[1,1,1024,768]{2,3,1,0:T(8,128)(2,1)}, bf16[1,1,1024,768]{2,3,1,0:T(8,128)(2,1)S(1)}, u32[]{:S(2)}) copy-start(bf16[1,1,1024,768]{2,3,1,0:T(8,128)(2,1)S(1)} %get-tuple-element.10) | copy-start | bytes 4718596
  50.2 22.7 %copy-start = (f32[1024,3072]{1,0:T(8,128)}, f32[1024,3072]{1,0:T(8,128)S(1)}, u32[]{:S(2)}) copy-start(f32[1024,3072]{1,0:T(8,128)S(1)} %fusion.49) | copy-start | bytes 37748740
  50.2 22.7 %copy-start.9 = (bf16[1,1024,768]{2,1,0:T(8,128)(2,1)S(1)}, bf16[1,1024,768]{2,1,0:T(8,128)(2,1)}, u32[]{:S(2)}) copy-start(bf16[1,1024,768]{2,1,0:T(8,128)(2,1)} %param.5) | copy-start | bytes 4718596
  84.8 142.6 %reduce-scatter.29.cloned.1.call-start = ((), (), s32[]{:S(2)}) async-start(), calls=%async_computation.14 | async-start | bytes 10027008
  86.5 24.1 %slice-start = ((s8[12582912]{0:T(1024)(128)(4,1)}), s8[4194304]{0:T(1024)(128)(4,1)S(1)}, s32[]{:S(2)}) async-start(s8[12582912]{0:T(1024)(128)(4,1)} %bitcast.343), calls=%async_computation.15 | async-start | bytes 8388608
  86.5 24.1 %slice-start.1 = ((s8[12582912]{0:T(1024)(128)(4,1)}), s8[4194304]{0:T(1024)(128)(4,1)S(1)}, s32[]{:S(2)}) async-start(s8[12582912]{0:T(1024)(128)(4,1)} %bitcast.343), calls=%async_computation.16 | async-start | bytes 8388608
  97.0 13.6 %slice-start.2 = ((s8[12582912]{0:T(1024)(128)(4,1)}), s8[4194304]{0:T(1024)(128)(4,1)S(1)}, s32[]{:S(2)}) async-start(s8[12582912]{0:T(1024)(128)(4,1)} %bitcast.343), calls=%async_computation.17 | async-start | bytes 8388608
  121.2 10.1 %copy-start.2 = (bf16[1,1,1024,768]{2,3,1,0:T(8,128)(2,1)S(1)}, bf16[1,1,1024,768]{2,3,1,0:T(8,128)(2,1)}, u32[]{:S(2)}) copy-start(bf16[1,1,1024,768]{2,3,1,0:T(8,128)(2,1)} %copy-done.1) | copy-start | bytes 4718596
  121.2 10.1 %copy-start.7 = (bf16[1,1024,768]{1,2,0:T(8,128)(2,1)S(1)}, bf16[1,1024,768]{1,2,0:T(8,128)(2,1)}, u32[]{:S(2)}) copy-start(bf16[1,1024,768]{1,2,0:T(8,128)(2,1)} %copy.1) | copy-start | bytes 4718596
  143.9 154.4 %reduce-scatter.23.cloned.1.call-start = ((), (), s32[]{:S(2)}) async-start(), calls=%async_computation.11 | async-start | bytes 10027008
  155.5 10.3 %copy-start.10 = (bf16[1,1024,768]{1,2,0:T(8,128)(2,1)S(1)}, bf16[1,1024,768]{1,2,0:T(8,128)(2,1)}, u32[]{:S(2)}) copy-start(bf16[1,1024,768]{1,2,0:T(8,128)(2,1)} %copy) | copy-start | bytes 4718596
  155.5 10.3 %copy-start.15 = (f32[1024]{0:T(1024)S(1)}, f32[1024]{0:T(1024)}, u32[]{:S(2)}) copy-start(f32[1024]{0:T(1024)} %copy-done.14) | copy-start | bytes 12292
  155.5 214.3 %reduce-scatter.25.cloned.1.call-start = ((), (), s32[]{:S(2)}) async-start(), calls=%async_computation.12 | async-start | bytes 10027008
  176.5 264.7 %reduce-scatter.19.cloned.1.call-start = ((), (), s32[]{:S(2)}) async-start(), calls=%async_computation.9 | async-start | bytes 10027008
  187.0 325.6 %reduce-scatter.21.cloned.1.call-start = ((), (), s32[]{:S(2)}) async-start(), calls=%async_computation.10 | async-start | bytes 10027008
  203.1 404.4 %all-gather.14.cloned.1.call-start = ((), (), s32[]{:S(2)}) async-start(), calls=%async_computation.8 | async-start | bytes 10027008 | tf_op jit(solution)/reshape | solution.py:58
  206.1 338.5 %copy-start.12 = (f32[2,192,768]{2,1,0:T(8,128)S(1)}, f32[2,192,768]{2,1,0:T(8,128)}, u32[]{:S(2)}) copy-start(f32[2,192,768]{2,1,0:T(8,128)} %param.10) | copy-start | bytes 3538948
  548.4 117.3 %all-gather.10.cloned.1.call-start = ((), (), s32[]{:S(2)}) async-start(), calls=%async_computation.6 | async-start | bytes 10027008 | tf_op jit(solution)/reshape | solution.py:58
  552.7 171.3 %all-gather.12.cloned.1.call-start = ((), (), s32[]{:S(2)}) async-start(), calls=%async_computation.7 | async-start | bytes 10027008 | tf_op jit(solution)/reshape | solution.py:58
  (6 other events, 15.9 us)
Sparse Core Ops, SparseCore 0:
  84.9 71.4 reduce-scatter.26
  158.8 68.6 reduce-scatter.28
  229.8 68.5 reduce-scatter.22
  301.1 68.5 reduce-scatter.24
  372.6 68.5 reduce-scatter.18
  443.9 68.5 reduce-scatter.20
  548.5 58.9 all-gather.13
  609.7 55.9 all-gather.9
  667.9 55.9 all-gather.11
where the time goes:
time: 761 us; the launch traced here: 755 us
  waiting for transfers between devices  468 us (61%)
  matrix products  163 us (21%)
  other arithmetic  41.9 us (6%)
  local copies, waits for them, and re-layouts  36.5 us (5%)
  blocking collectives  27.4 us (4%)
  between operations  17.7 us (2%)
    unnamed x15, waiting for transfers between devices  301 us
    reshape x3, waiting for transfers between devices, step(): t.reshape(-1, *t.shape[2:])  167 us
    dot_general x5, matrix products, layer(): up = jnp.dot(a, w['w_up'], preferred_element_type=jnp.float32)  64.1 us
    dot_general x5, matrix products, layer(): gate = jnp.dot(a, w['w_gate'], preferred_element_type=jnp.float32)  51.1 us
    dot_general x5, matrix products, matmul(): jnp.dot(a, w, preferred_element_type=jnp.float32).astype(jnp.bfloat16)  47.9 us
    unnamed x47, local copies, waits for them, and re-layouts  35.9 us
    reduce_sum x1, blocking collectives, of_a_group(): jnp.sum(g * g)  27.4 us
    unnamed x4, other arithmetic  19.2 us
  transfers between devices with their start and end apart: 9, of which 8 were waited for; matrix products, arithmetic and copies ran while one was open for 17% of the time, Pallas kernels for 0%

commit v1 on v0

v1 whole, which is shorter than its diff:
```python
import functools

import jax
import jax.numpy as jnp
from jax import lax
from jax.experimental import pallas as pl
from jax.experimental.pallas import tpu as pltpu
from jax.sharding import PartitionSpec as P

F32, BF16 = jnp.float32, jnp.bfloat16
ANY, VMEM = pl.ANY, pltpu.VMEM
MESH = pl.DeviceIdType.MESH
VMEM_BYTES = 64 * 1024 * 1024 - 65536


def remote(src, dst, send, recv, to):
    return pltpu.make_async_remote_copy(
        src_ref=src, dst_ref=dst, send_sem=send, recv_sem=recv, device_id={"dp": to}, device_id_type=MESH
    )


def enter(peers):
    barrier = pltpu.get_barrier_semaphore()
    for peer in peers:
        pl.semaphore_signal(barrier, inc=1, device_id={"dp": peer}, device_id_type=MESH)
    pl.semaphore_wait(barrier, len(peers))


def sum_kernel(n, sources, *refs):
    inputs = refs[: len(sources)]
    g_ref, total_ref = refs[len(sources) : len(sources) + 2]
    (a_buf, b_buf, mine, theirs, ring, squares, slots, load_sem, swap_send, swap_recv, ring_send, ring_recv, all_send, all_recv) = refs[
        len(sources) + 2 :
    ]
    d = a_buf.shape[2]
    r, ff = mine.shape[2:]
    half, tiles, chips = ff // 2, ff // d, n // 2
    count = ring.shape[0]
    pairs = count // 2
    me = lax.axis_index("dp")
    z, c = lax.div(me, 2), lax.rem(me, 2)
    partner = 2 * z + 1 - c
    right = 2 * lax.rem(z + 1, chips) + c
    left = 2 * lax.rem(z + chips - 1, chips) + c
    onward = (right, left)

    def loads(k, t, slot):
        a, b, a_moves = sources_of[k]
        moving = pl.ds(pl.multiple_of(t * d, d), d)
        whole = pl.ds(0, d)
        return (
            pltpu.make_async_copy(a.at[:, moving if a_moves else whole], a_buf.at[slot], load_sem.at[slot, 0]),
            pltpu.make_async_copy(b.at[:, whole if a_moves else moving], b_buf.at[slot], load_sem.at[slot, 1]),
        )

    sources_of = [(inputs[ia], inputs[ib], moves) for ia, ib, moves in SOURCES]

    def start_load(index):
        for k in range(count):

            @pl.when(lax.div(index, tiles) == k)
            def _():
                for copy in loads(k, lax.rem(index, tiles), lax.rem(index, 2)):
                    copy.start()

    def swap(k):
        return remote(mine.at[4 + lax.rem(k, 2)], theirs.at[k], swap_send.at[k], swap_recv.at[k], partner)

    def hop(k, way, s):
        return remote(ring.at[k, way, s], ring.at[k, way, s + 1], ring_send.at[k, way, s], ring_recv.at[k, way, s], onward[way])

    def tile(index):
        k, t, slot = lax.div(index, tiles), lax.rem(index, tiles), lax.rem(index, 2)

        @pl.when(index + 1 < count * tiles)
        def _():
            start_load(index + 1)

        @pl.when(jnp.logical_and(t == 0, k >= 2))
        def _():
            swap(k - 2).wait_send()

        for copy in loads(0, 0, slot):
            copy.wait()
        down = 1 - lax.div(lax.rem(k, 3) + 1, 2)
        for part in range(2):
            cols = d // 2
            out = lax.dot_general(
                a_buf[slot, :, part * cols : (part + 1) * cols], b_buf[slot], (((0,), (0,)), ((), ())), preferred_element_type=F32
            ).astype(BF16)
            for i in range(cols // r):
                group = part * (cols // r) + i
                device = down * (t * (n // tiles) + group // tiles) + (1 - down) * group
                at = down * ((group % tiles) * d) + (1 - down) * (t * d)
                same = 1 - lax.rem(lax.rem(device, 2) + c, 2)
                buf = same * lax.rem(k, 4) + (1 - same) * (4 + lax.rem(k, 2))
                mine[buf, lax.div(device, 2), :, pl.ds(pl.multiple_of(at, d), d)] = out[i * r : (i + 1) * r]

        @pl.when(t == tiles - 1)
        def _():
            swap(k).start()

    def term(k, way, chip):
        cols = slice(way * half, (way + 1) * half)
        return mine[lax.rem(k, 4), chip, :, cols].astype(F32) + theirs[k, chip, :, cols].astype(F32)

    def meant_for(way, s):
        return lax.rem(z + chips - 1 - s, chips) if way == 0 else lax.rem(z + 1 + s, chips)

    def first(k):
        swap(k).wait_recv()
        for way in range(2):
            ring[k, way, 0] = term(k, way, meant_for(way, 0)).astype(BF16)
            hop(k, way, 0).start()

    def middle(k, s):
        for way in range(2):
            hop(k, way, s - 1).wait_recv()
            ring[k, way, s] = (term(k, way, meant_for(way, s)) + ring[k, way, s].astype(F32)).astype(BF16)
            hop(k, way, s).start()

    def last(k):
        for way in range(2):
            hop(k, way, chips - 2).wait_recv()
            g = (term(k, way, z) + ring[k, way, chips - 1].astype(F32)).astype(BF16)
            g_ref[k, :, way * half : (way + 1) * half] = g
            squares[...] += g.astype(F32) * g.astype(F32)

    start_load(0)
    squares[...] = jnp.zeros_like(squares)
    enter([lax.rem(me + o, n) for o in range(1, n)])

    @pl.loop(0, pairs + 1)
    def _(ii):
        @pl.loop(0, chips - 1)
        def _(s):
            for j in range(2):
                k = 2 * (ii - 1) + j

                @pl.when(jnp.logical_and(ii > 0, s == 0))
                def _():
                    first(k)

                @pl.when(jnp.logical_and(ii > 0, s > 0))
                def _():
                    middle(k, s)

                @pl.when(jnp.logical_and(ii > 1, s == 0))
                def _():
                    last(k - 2)

                @pl.when(jnp.logical_and(ii < pairs, s < tiles))
                def _():
                    tile(2 * tiles * ii + 2 * s + j)

    for j in range(2):
        last(jnp.int32(count - 2 + j))

    whole = squares[0:8, 0:128]
    for i in range(r // 8):
        for q in range(half // 128):
            if i or q:
                whole = whole + squares[i * 8 : (i + 1) * 8, q * 128 : (q + 1) * 128]
    slots[0] = whole
    sends = [remote(slots.at[0], slots.at[o], all_send.at[o], all_recv.at[o], lax.rem(me + o, n)) for o in range(1, n)]
    for send in sends:
        send.start()
    for send in sends:
        send.wait_recv()
    whole = slots[0]
    for o in range(1, n):
        whole = whole + slots[o]
    total_ref[...] = jnp.full(total_ref.shape, jnp.sum(whole), F32)
    for send in sends:
        send.wait_send()

    @pl.loop(0, count)
    def _(k):
        @pl.loop(0, chips - 1)
        def _(s):
            for way in range(2):
                hop(k, way, s).wait_send()

    for j in range(2):
        swap(jnp.int32(count - 2 + j)).wait_send()


SOURCES = ((0, 4, True), (1, 2, False), (1, 3, False), (5, 9, True), (6, 7, False), (6, 8, False))


def summed(n, arrays):
    tokens, d = arrays[1].shape
    ff = arrays[0].shape[1]
    r, chips, count = d // n, n // 2, len(SOURCES)
    dma = pltpu.SemaphoreType.DMA
    return pl.pallas_call(
        functools.partial(sum_kernel, n, arrays),
        out_shape=(jax.ShapeDtypeStruct((count, r, ff), BF16), jax.ShapeDtypeStruct((8, 128), F32)),
        in_specs=[pl.BlockSpec(memory_space=ANY)] * len(arrays),
        out_specs=(pl.BlockSpec(memory_space=VMEM), pl.BlockSpec(memory_space=VMEM)),
        scratch_shapes=[
            VMEM((2, tokens, d), BF16),
            VMEM((2, tokens, d), BF16),
            VMEM((6, chips, r, ff), BF16),
            VMEM((count, chips, r, ff), BF16),
            VMEM((count, 2, chips, r, ff // 2), BF16),
            VMEM((r, ff // 2), F32),
            VMEM((n, 8, 128), F32),
            dma((2, 2)),
            dma((count,)),
            dma((count,)),
            dma((count, 2, chips - 1)),
            dma((count, 2, chips - 1)),
            dma((n,)),
            dma((n,)),
        ],
        compiler_params=pltpu.CompilerParams(collective_id=0, has_side_effects=True, vmem_limit_bytes=VMEM_BYTES),
        name="gradient_sum",
    )(*arrays)


WEIGHTS = ((2, 1), (0, 1), (1, 1), (2, 0), (0, 0), (1, 0))


def pieces(k, array, block):
    name, layer = WEIGHTS[k]
    if name < 2:
        return [(array.at[layer], block)]
    tiles, width = array.shape[-3], array.shape[-1]
    lead = (slice(None),) * (len(array.shape) - 4)
    return [(array.at[(layer, *lead, q)], block.at[(*lead, slice(None), pl.ds(q * width, width))]) for q in range(tiles)]


def own_pieces(k, array, block, me):
    name, layer = WEIGHTS[k]
    if name < 2:
        return [(array.at[layer, me], block)]
    tiles, width = array.shape[-3], array.shape[-1]
    return [(array.at[layer, me, q], block.at[:, pl.ds(q * width, width)]) for q in range(tiles)]


def gather_kernel(n, g_ref, total_ref, *refs):
    w_in, m_in, v_in = (refs[i : i + 3] for i in range(0, 9, 3))
    count, r, ff = g_ref.shape
    w_out = refs[9 : 9 + count]
    m_out, v_out, w_buf, m_buf, v_buf, load_sem, store_sem, ring_send, ring_recv, pair_send, pair_recv = refs[9 + count :]
    half, chunk, chips = ff // 2, ff // 4, n // 2
    me = lax.axis_index("dp")
    z, c = lax.div(me, 2), lax.rem(me, 2)
    partner = 2 * z + 1 - c
    right = 2 * lax.rem(z + 1, chips) + c
    left = 2 * lax.rem(z + chips - 1, chips) + c
    onward = (right, left)

    def loads(k):
        name = WEIGHTS[k][0]
        parts = own_pieces(k, w_in[name], w_buf.at[k], me) + pieces(k, m_in[name], m_buf.at[k]) + pieces(k, v_in[name], v_buf.at[k])
        return [pltpu.make_async_copy(src, dst, load_sem.at[k, i]) for i, (src, dst) in enumerate(parts)]

    def stores(k):
        return (
            pltpu.make_async_copy(w_buf.at[k], w_out[k].at[me], store_sem.at[k, 0]),
            pltpu.make_async_copy(m_buf.at[k], m_out.at[k], store_sem.at[k, 1]),
            pltpu.make_async_copy(v_buf.at[k], v_out.at[k], store_sem.at[k, 2]),
        )

    def came(way, s):
        return lax.rem(z + chips - s, chips) if way == 0 else lax.rem(z + s, chips)

    def part(k, way, s):
        return w_out[k].at[2 * came(way, s) + c, :, pl.ds(way * half, half)]

    def hop(k, way, s, source=None):
        ref = part(k, way, s)
        return remote(ref if source is None else source, ref, ring_send.at[k, way, s], ring_recv.at[k, way, s], onward[way])

    def across(k, way, s, source=None):
        ref = part(k, way, s)
        return remote(ref if source is None else source, ref, pair_send.at[k, way, s], pair_recv.at[k, way, s], partner)

    for k in range(count):
        for copy in loads(k):
            copy.start()
    enter((partner, left, right))
    factor = jnp.minimum(1.0, 0.5 * lax.rsqrt(total_ref[0:1, 0:1] * (1.0 / (count * r * ff * n)) + 1e-30))

    for k in range(count):
        for copy in loads(k):
            copy.wait()

        @pl.loop(0, ff // chunk)
        def _(q):
            cols = pl.ds(pl.multiple_of(q * chunk, chunk), chunk)
            g = g_ref[k, :, cols].astype(F32) * factor
            m = 0.9 * m_buf[k, :, cols] + 0.1 * g
            v = 0.95 * v_buf[k, :, cols] + 0.05 * g * g
            w = w_buf[k, :, cols].astype(F32)
            step = m * lax.rsqrt(v + 1e-8) + 0.1 * w
            m_buf[k, :, cols] = m
            v_buf[k, :, cols] = v
            w_buf[k, :, cols] = (w - 0.02 * step).astype(BF16)

        for way in range(2):
            own = w_buf.at[k, :, pl.ds(way * half, half)]
            hop(k, way, 0, own).start()
            across(k, way, 0, own).start()
        for copy in stores(k):
            copy.start()

    @pl.loop(1, chips)
    def _(s):
        for k in range(count):
            for way in range(2):
                hop(k, way, s - 1).wait_recv()

                @pl.when(s < chips - 1)
                def _():
                    hop(k, way, s).start()

                across(k, way, s).start()

    for k in range(count):
        for copy in stores(k):
            copy.wait()

        @pl.loop(0, chips)
        def _(s):
            for way in range(2):
                across(k, way, s).wait()

                @pl.when(s < chips - 1)
                def _():
                    hop(k, way, s).wait_send()


def stepped(n, g, total, w, m, v):
    count, r, ff = g.shape
    layers, d = w[0].shape[:2]
    chips, tiles = n // 2, ff // d
    dma = pltpu.SemaphoreType.DMA
    any_spec, vmem_spec = pl.BlockSpec(memory_space=ANY), pl.BlockSpec(memory_space=VMEM)
    row = (layers, r, ff), (layers, r, ff), (layers, tiles, r, d)
    whole = (layers, n, r, ff), (layers, n, r, ff), (layers, n, tiles, r, d)
    w = [t.reshape(s) for t, s in zip(w, whole, strict=True)]
    m, v = ([t.reshape(s) for t, s in zip(ts, row, strict=True)] for ts in (m, v))
    held = pl.pallas_call(
        functools.partial(gather_kernel, n),
        out_shape=(*[VMEM((n, r, ff), BF16)] * count, VMEM((count, r, ff), F32), VMEM((count, r, ff), F32)),
        in_specs=[vmem_spec] * 2 + [any_spec] * 9,
        out_specs=(any_spec,) * (count + 2),
        scratch_shapes=[
            *[VMEM((count, r, ff), t) for t in (BF16, F32, F32)],
            dma((count, 3 * tiles)),
            dma((count, 3)),
            *[dma((count, 2, chips - 1)) for _ in range(2)],
            *[dma((count, 2, chips)) for _ in range(2)],
        ],
        compiler_params=pltpu.CompilerParams(collective_id=1, has_side_effects=True, vmem_limit_bytes=20 * 1024 * 1024),
        name="step_and_gather",
    )(g, total, *w, *m, *v)

    def write_out(*refs):
        w_held, (m_held, v_held, *outs, sem) = refs[:count], refs[count:]
        parts = [
            pair
            for k, (name, _) in enumerate(WEIGHTS)
            for out, block in ((outs[name], w_held[k]), (outs[3 + name], m_held.at[k]), (outs[6 + name], v_held.at[k]))
            for pair in pieces(k, out, block)
        ]
        copies = [pltpu.make_async_copy(block, out, sem.at[i]) for i, (out, block) in enumerate(parts)]
        for copy in copies:
            copy.start()
        for copy in copies:
            copy.wait()

    outs = pl.pallas_call(
        write_out,
        out_shape=tuple(jax.ShapeDtypeStruct(t.shape, t.dtype) for t in (*w, *m, *v)),
        in_specs=[any_spec] * (count + 2),
        out_specs=(any_spec,) * 9,
        scratch_shapes=[dma((3 * count * tiles,))],
        compiler_params=pltpu.CompilerParams(vmem_limit_bytes=1024 * 1024),
        name="write_out",
    )(*held)
    rows = (layers, d, ff), (layers, d, ff), (layers, ff, d)
    blocks = (layers, r, ff), (layers, r, ff), (layers, tiles * r, d)
    return [t.reshape(s) for t, s in zip(outs, (*rows, *blocks, *blocks), strict=True)]


def normed(h):
    wide = h.astype(F32)
    scale = lax.rsqrt(jnp.mean(wide**2, -1, keepdims=True) + 1e-6)
    return (wide * scale).astype(BF16)


def back_through_norm(h, da):
    wide, g = h.astype(F32), da.astype(F32)
    mean = jnp.mean(wide**2, -1, keepdims=True) + 1e-6
    scale = lax.rsqrt(mean)
    inner = jnp.mean(g * wide, -1, keepdims=True)
    return (scale * g - wide * (inner * scale / mean)).astype(BF16)


def back_through_product(gate, up, s, dhid):
    p = dhid.astype(BF16).astype(F32)
    return (p * up * (s * (1 + gate * (1 - s)))).astype(BF16), (p * (gate * s)).astype(BF16)


def dot(a, b):
    return jnp.dot(a, b, preferred_element_type=F32)


def dot_t(a, b):
    return lax.dot_general(a, b, (((1,), (1,)), ((), ())), preferred_element_type=F32)


def forward_kernel(chunks, x_ref, wg_ref, wu_ref, wd_ref, a_ref, hid_ref, gate_ref, up_ref, h_ref, acc):
    i = pl.program_id(0)
    size = x_ref.shape[0] // chunks

    @pl.when(i == 0)
    def _():
        a_ref[...] = normed(x_ref[...])

    for q in range(chunks):
        rows = slice(q * size, (q + 1) * size)
        gate, up = dot(a_ref[rows], wg_ref[...]), dot(a_ref[rows], wu_ref[...])
        hid = (gate * jax.nn.sigmoid(gate) * up).astype(BF16)
        gate_ref[rows], up_ref[rows], hid_ref[rows] = gate, up, hid
        more = dot(hid, wd_ref[...])

        @pl.when(i == 0)
        def _():
            acc[rows] = more

        @pl.when(i > 0)
        def _():
            acc[rows] += more

    @pl.when(i == pl.num_programs(0) - 1)
    def _():
        h_ref[...] = x_ref[...] + acc[...].astype(BF16)


def turn_kernel(chunks, h_ref, dy_ref, wg_ref, wu_ref, wd_ref, a_ref, hid_ref, dgate_ref, dup_ref, dh_ref, acc_g, acc_u):
    i = pl.program_id(0)
    size = h_ref.shape[0] // chunks

    @pl.when(i == 0)
    def _():
        a_ref[...] = normed(h_ref[...])
        acc_g[...] = jnp.zeros_like(acc_g)
        acc_u[...] = jnp.zeros_like(acc_u)

    for q in range(chunks):
        rows = slice(q * size, (q + 1) * size)
        gate, up = dot(a_ref[rows], wg_ref[...]), dot(a_ref[rows], wu_ref[...])
        dhid = dot_t(dy_ref[rows], wd_ref[...])
        s = jax.nn.sigmoid(gate)
        hid_ref[rows] = (gate * s * up).astype(BF16)
        dgate, dup = back_through_product(gate, up, s, dhid)
        dgate_ref[rows], dup_ref[rows] = dgate, dup
        acc_g[rows] += dot_t(dgate, wg_ref[...])
        acc_u[rows] += dot_t(dup, wu_ref[...])

    @pl.when(i == pl.num_programs(0) - 1)
    def _():
        da = acc_g[...].astype(BF16) + acc_u[...].astype(BF16)
        dh_ref[...] = dy_ref[...] + back_through_norm(h_ref[...], da)


def back_kernel(chunks, dy_ref, gate_ref, up_ref, wd_ref, dgate_ref, dup_ref):
    size = dy_ref.shape[0] // chunks
    for q in range(chunks):
        rows = slice(q * size, (q + 1) * size)
        gate = gate_ref[rows]
        dgate_ref[rows], dup_ref[rows] = back_through_product(gate, up_ref[rows], jax.nn.sigmoid(gate), dot_t(dy_ref[rows], wd_ref[...]))


def operands(x, dy, w_gate, w_up, w_down):
    (tokens, d), ff = x.shape, w_gate.shape[2]
    tile, chunks = ff // 6, 4
    grid = (ff // tile,)
    like = jax.ShapeDtypeStruct
    state, states = pl.BlockSpec((tokens, d), lambda i: (0, 0)), like((tokens, d), BF16)
    hidden, hiddens, wide = pl.BlockSpec((tokens, tile), lambda i: (0, i)), like((tokens, ff), BF16), like((tokens, ff), F32)

    def into(layer):
        return pl.BlockSpec((None, d, tile), lambda i: (layer, 0, i))

    def out_of(layer):
        return pl.BlockSpec((None, tile, d), lambda i: (layer, i, 0))

    acc = VMEM((tokens, d), F32)
    params = pltpu.CompilerParams(vmem_limit_bytes=56 * 1024 * 1024, dimension_semantics=("arbitrary",))
    a0, hid0, gate0, up0, h1 = pl.pallas_call(
        functools.partial(forward_kernel, chunks),
        grid=grid,
        out_shape=(states, hiddens, wide, wide, states),
        in_specs=[state, into(0), into(0), out_of(0)],
        out_specs=(state, hidden, hidden, hidden, state),
        scratch_shapes=[acc],
        compiler_params=params,
        name="first_forward",
    )(x, w_gate, w_up, w_down)
    a1, hid1, dgate1, dup1, dy0 = pl.pallas_call(
        functools.partial(turn_kernel, chunks),
        grid=grid,
        out_shape=(states, hiddens, hiddens, hiddens, states),
        in_specs=[state, state, into(1), into(1), out_of(1)],
        out_specs=(state, hidden, hidden, hidden, state),
        scratch_shapes=[acc, acc],
        compiler_params=params,
        name="last_layer",
    )(h1, dy, w_gate, w_up, w_down)
    dgate0, dup0 = pl.pallas_call(
        functools.partial(back_kernel, chunks),
        grid=grid,
        out_shape=(hiddens, hiddens),
        in_specs=[state, hidden, hidden, out_of(0)],
        out_specs=(hidden, hidden),
        compiler_params=params,
        name="first_back",
    )(dy0, gate0, up0, w_down)
    return hid1, a1, dgate1, dup1, dy, hid0, a0, dgate0, dup0, dy0


def solution(mesh):
    n = mesh.shape["dp"]

    def device(x, dy, *arrays):
        w, m, v = (arrays[i : i + 3] for i in (0, 3, 6))
        g, total = summed(n, operands(x[0], dy[0], *w))
        return tuple(stepped(n, g, total, w, m, v))

    whole, rows = P(None, None, None), P(None, "dp", None)
    tokens = P(("rep", "dp"), None, None)
    return jax.shard_map(
        device,
        mesh=mesh,
        in_specs=(tokens, tokens, *[whole] * 3, *[rows] * 6),
        out_specs=(*[P("rep", None, None)] * 3, *[P("rep", "dp", None)] * 6),
        check_vma=False,
    )
```

time: 761 us -> 422 us (0.55)
  waiting for transfers between devices: 468 us -> 0 us
  Pallas kernels: 0 us -> 411 us
  matrix products: 163 us -> 0 us
  other arithmetic: 41.9 us -> 0 us
  blocking collectives: 27.4 us -> 0 us
  local copies, waits for them, and re-layouts: 36.5 us -> 9.72 us
  between operations: 17.7 us -> 0.85 us
    pallas_call x0 -> x6, Pallas kernels: none -> 411 us  [the longest x1 169 us: summed(): pl.pallas_call(functools.partial(sum_kernel, n, arrays), out_shape=(jax.S...]
    unnamed x15 -> x0, waiting for transfers between devices: 301 us -> none
    reshape x3 -> x0, waiting for transfers between devices: 167 us -> none  [step(): t.reshape(-1, *t.shape[2:])]
    dot_general x15 -> x0, matrix products: 163 us -> none  [the longest x5 64.1 us: layer(): up = jnp.dot(a, w['w_up'], preferred_element_type=jnp.float32)]
    reduce_sum x1 -> x0, blocking collectives: 27.4 us -> none  [of_a_group(): jnp.sum(g * g)]
    unnamed x47 -> x10, local copies, waits for them, and re-layouts: 35.9 us -> 9.72 us
    unnamed x4 -> x0, other arithmetic: 19.2 us -> none
    reshape x3 -> x0, other arithmetic: 11.5 us -> none  [step(): t.reshape(-1, *t.shape[2:])]
  transfers between devices with their start and end apart: 9 -> 0, of which waited for: 8 -> 0; matrix products, arithmetic and copies ran while one was open for 17% -> 0% of each run, Pallas kernels for 0% -> 0%
where the time goes in v1:
time: 422 us
  Pallas kernels  411 us (97%)
  local copies, waits for them, and re-layouts  9.72 us (2%)
    pallas_call x1, Pallas kernels, summed(): pl.pallas_call(functools.partial(sum_kernel, n, arrays), out_shape=(jax.S...  169 us
    pallas_call x1, Pallas kernels, stepped(): pl.pallas_call(functools.partial(gather_kernel, n), out_shape=(*[VMEM((n,...  144 us
    pallas_call x1, Pallas kernels, operands(): pl.pallas_call(functools.partial(turn_kernel, chunks), grid=grid, out_sha...  37.2 us
    pallas_call x1, Pallas kernels, operands(): pl.pallas_call(functools.partial(forward_kernel, chunks), grid=grid, out_...  30.8 us
    pallas_call x1, Pallas kernels, operands(): pl.pallas_call(functools.partial(back_kernel, chunks), grid=grid, out_sha...  18.4 us
    pallas_call x1, Pallas kernels, stepped(): pl.pallas_call(write_out, out_shape=tuple((jax.ShapeDtypeStruct(t.shape,...  12.1 us
    unnamed x10, local copies, waits for them, and re-layouts  9.72 us

profile of v1, /device:TPU:21, one launch (start us, length us, event | category | flops | bytes accessed | tf_op | source)
XLA Modules:
  0.0 422.0 jit_solution(13492195750536260907)
XLA Ops:
  0.6 30.8 %first_forward.1 = (bf16[1024,768]{1,0:T(8,128)(2,1)}, bf16[1024,3072]{1,0:T(8,128)(2,1)}, f32[1024,3072]{1,0:T(8,128)}, f32[1024,3072]{1,0:T(8,128)}, bf16[1024,768]{1,0:T(8,128)(2,1)}) custom-call(bf16[1024,768]{1,0:T(8,128)(2,1)} %bitcast.17, bf16[2,768,3072]{2,1,0:T(8,128)(2,1)} %wg_ref.3, bf16[2,768,3072]{2,1,0:T(8,128)(2,1)} %wu_ref.3, ...), custom_call_target="tpu_custom_call" | custom-call | tf_op jit(solution)/shard_map/first_forward/pallas_call | solution.py:496
  31.5 37.2 %last_layer.1 = (bf16[1024,768]{1,0:T(8,128)(2,1)}, bf16[1024,3072]{1,0:T(8,128)(2,1)}, bf16[1024,3072]{1,0:T(8,128)(2,1)}, bf16[1024,3072]{1,0:T(8,128)(2,1)}, bf16[1024,768]{1,0:T(8,128)(2,1)}) custom-call(bf16[1024,768]{1,0:T(8,128)(2,1)} %get-tuple-element.40.h_ref, bf16[1024,768]{1,0:T(8,128)(2,1)} %bitcast.15, bf16[2,768,3072]{2,1,0:T(8,128)(2,1)} %wg_ref.3, ...), custom_call_target="tpu_custom_call" | custom-call | tf_op jit(solution)/shard_map/last_layer/pallas_call | solution.py:506
  68.7 18.4 %first_back.1 = (bf16[1024,3072]{1,0:T(8,128)(2,1)}, bf16[1024,3072]{1,0:T(8,128)(2,1)}) custom-call(bf16[1024,768]{1,0:T(8,128)(2,1)} %get-tuple-element.47.dy_ref.refs_9_, f32[1024,3072]{1,0:T(8,128)} %get-tuple-element.48.gate_ref, f32[1024,3072]{1,0:T(8,128)} %get-tuple-element.49.up_ref, bf16[2,3072,768]{2,1,0:T(8,128)(2,1)} %wd_ref.5), custom_call_target="tpu_custom_call" | custom-call | tf_op jit(solution)/shard_map/first_back/pallas_call | solution.py:516
  87.1 168.7 %gradient_sum.1 = (bf16[6,48,3072]{2,1,0:T(8,128)(2,1)}, f32[8,128]{1,0:T(8,128)}) custom-call(bf16[1024,3072]{1,0:T(8,128)(2,1)} %get-tuple-element.41.refs_0_, bf16[1024,768]{1,0:T(8,128)(2,1)} %get-tuple-element.42.refs_1_, bf16[1024,3072]{1,0:T(8,128)(2,1)} %get-tuple-element.43.refs_2_, bf16[1024,3072]{1,0:T(8,128)(2,1)} %get-tuple-element.44.refs_3_, ...), custom_call_target="tpu_custom_call" | custom-call | tf_op jit(solution)/shard_map/gradient_sum/pallas_call | solution.py:196
  255.8 0.0 copy-start.4
  255.8 0.7 copy-done.4
  256.5 144.3 %step_and_gather.1 = (bf16[16,48,3072]{2,1,0:T(8,128)(2,1)S(1)}, bf16[16,48,3072]{2,1,0:T(8,128)(2,1)S(1)}, bf16[16,48,3072]{2,1,0:T(8,128)(2,1)S(1)}, bf16[16,4...) custom-call(bf16[6,48,3072]{2,1,0:T(8,128)(2,1)} %get-tuple-element., ...), custom_call_target="tpu_custom_call" | custom-call | tf_op jit(solution)/shard_map/step_and_gather/pallas_call | solution.py:346
  400.7 0.0 copy-start
  400.8 2.2 copy-done
  402.9 0.0 copy-start.2
  402.9 2.2 copy-done.2
  405.1 0.0 copy-start.1
  405.1 2.3 copy-done.1
  407.5 0.0 copy-start.3
  407.5 2.3 copy-done.3
  409.8 12.1 %write_out.1 = (bf16[2,16,48,3072]{3,2,1,0:T(8,128)(2,1)}, bf16[2,16,48,3072]{3,2,1,0:T(8,128)(2,1)}, bf16[2,16,4,48,768]{4,3,2,1,0:T(8,128)(2,1)}, f32[2,48,307...) custom-call(bf16[16,48,3072]{2,1,0:T(8,128)(2,1)S(1)} %get-tuple-ele, ...), custom_call_target="tpu_custom_call" | custom-call | tf_op jit(solution)/shard_map/write_out/pallas_call | solution.py:376
Async XLA Ops:
  255.8 0.7 copy-start.4
  400.7 2.2 copy-start
  402.9 2.2 copy-start.2
  405.1 2.3 copy-start.1
  407.5 2.3 copy-start.3

commit v2 on v1

--- a/solution.py
+++ b/solution.py
@@ -26,15 +26,19 @@
     pl.semaphore_wait(barrier, len(peers))
 
 
-def sum_kernel(n, sources, *refs):
-    inputs = refs[: len(sources)]
-    g_ref, total_ref = refs[len(sources) : len(sources) + 2]
-    (a_buf, b_buf, mine, theirs, ring, squares, slots, load_sem, swap_send, swap_recv, ring_send, ring_recv, all_send, all_recv) = refs[
-        len(sources) + 2 :
-    ]
+def sum_kernel(n, inputs_count, *refs):
+    *inputs, wg, wu, wd = refs[:inputs_count]
+    g_ref, total_ref, dgate, dup = refs[inputs_count : inputs_count + 4]
+    (a_buf, b_buf, wg_buf, wu_buf, wd_buf, mine, theirs, ring, squares, slots, *sems) = refs[inputs_count + 4 :]
+    load_sem, back_sem, swap_send, swap_recv, ring_send, ring_recv, all_send, all_recv = sems
+    inputs += [dgate, dup]
     d = a_buf.shape[2]
     r, ff = mine.shape[2:]
     half, tiles, chips = ff // 2, ff // d, n // 2
+    width = wg_buf.shape[1]
+    backs = ff // width
+    late = backs - (chips - 1 - tiles)
+    shift = 2 * late - 1
     count = ring.shape[0]
     pairs = count // 2
     me = lax.axis_index("dp")
@@ -55,6 +59,60 @@
 
     sources_of = [(inputs[ia], inputs[ib], moves) for ia, ib, moves in SOURCES]
 
+    def back_loads(u):
+        at = pl.ds(pl.multiple_of(u * width, width), width)
+        return (
+            pltpu.make_async_copy(wg.at[0, :, at], wg_buf, back_sem.at[0]),
+            pltpu.make_async_copy(wu.at[0, :, at], wu_buf, back_sem.at[1]),
+            pltpu.make_async_copy(wd.at[0, at], wd_buf, back_sem.at[2]),
+        )
+
+    def back_states():
+        return (
+            pltpu.make_async_copy(inputs[A0], a_buf.at[0], back_sem.at[3]),
+            pltpu.make_async_copy(inputs[DY0], b_buf.at[0], back_sem.at[4]),
+        )
+
+    def back_stores(u):
+        at = pl.ds(pl.multiple_of(u * width, width), width)
+        return (
+            pltpu.make_async_copy(a_buf.at[1, :, pl.ds(0, width)], dgate.at[:, at], back_sem.at[5]),
+            pltpu.make_async_copy(b_buf.at[1, :, pl.ds(0, width)], dup.at[:, at], back_sem.at[6]),
+        )
+
+    def back(u):
+        @pl.when(u == 0)
+        def _():
+            for copy in back_states():
+                copy.wait()
+
+        @pl.when(u > 0)
+        def _():
+            for copy in back_stores(u - 1):
+                copy.wait()
+
+        for copy in back_loads(u):
+            copy.wait()
+        size = a_buf.shape[1] // 4
+        for q in range(4):
+            rows = slice(q * size, (q + 1) * size)
+            gate, up = dot(a_buf[0, rows], wg_buf[...]), dot(a_buf[0, rows], wu_buf[...])
+            dhid = dot_t(b_buf[0, rows], wd_buf[...])
+            a_buf[1, rows, :width], b_buf[1, rows, :width] = back_through_product(gate, up, jax.nn.sigmoid(gate), dhid)
+        for copy in back_stores(u):
+            copy.start()
+
+        @pl.when(u + 1 < backs)
+        def _():
+            for copy in back_loads(u + 1):
+                copy.start()
+
+        @pl.when(u + 1 == backs)
+        def _():
+            for copy in back_stores(u):
+                copy.wait()
+            start_load(jnp.int32(2 * tiles * 2))
+
     def start_load(index):
         for k in range(count):
 
@@ -72,9 +130,14 @@
     def tile(index):
         k, t, slot = lax.div(index, tiles), lax.rem(index, tiles), lax.rem(index, 2)
 
-        @pl.when(index + 1 < count * tiles)
+        @pl.when(jnp.logical_and(index + 1 < count * tiles, index + 1 != 4 * tiles))
         def _():
             start_load(index + 1)
+
+        @pl.when(index + 1 == 4 * tiles)
+        def _():
+            for copy in back_loads(jnp.int32(0)):
+                copy.start()
 
         @pl.when(jnp.logical_and(t == 0, k >= 2))
         def _():
@@ -149,9 +212,28 @@
                 def _():
                     last(k - 2)
 
-                @pl.when(jnp.logical_and(ii < pairs, s < tiles))
+                place = 2 * s + j - shift * lax.div(ii, 2)
+
+                @pl.when(jnp.logical_and(ii < pairs, jnp.logical_and(place >= 0, place < 2 * tiles)))
                 def _():
-                    tile(2 * tiles * ii + 2 * s + j)
+                    tile(2 * tiles * ii + place)
+
+                if j == 0:
+
+                    @pl.when(jnp.logical_and(ii == 1, s == tiles))
+                    def _():
+                        for copy in back_states():
+                            copy.start()
+
+                if j == 0:
+                    due, u = jnp.logical_and(ii == 2, s == late - 1), jnp.int32(backs - 1)
+                else:
+                    due = jnp.logical_or(jnp.logical_and(ii == 1, s >= tiles), jnp.logical_and(ii == 2, s < late - 1))
+                    u = s - tiles + (ii - 1) * (chips - 1)
+
+                @pl.when(due)
+                def _():
+                    back(u)
 
     for j in range(2):
         last(jnp.int32(count - 2 + j))
@@ -185,28 +267,35 @@
         swap(jnp.int32(count - 2 + j)).wait_send()
 
 
-SOURCES = ((0, 4, True), (1, 2, False), (1, 3, False), (5, 9, True), (6, 7, False), (6, 8, False))
-
-
-def summed(n, arrays):
+SOURCES = ((0, 4, True), (1, 2, False), (1, 3, False), (5, 7, True), (6, 8, False), (6, 9, False))
+A0, DY0 = 6, 7
+
+
+def summed(n, arrays, weights):
     tokens, d = arrays[1].shape
     ff = arrays[0].shape[1]
-    r, chips, count = d // n, n // 2, len(SOURCES)
+    r, chips, count, width = d // n, n // 2, len(SOURCES), ff // 6
     dma = pltpu.SemaphoreType.DMA
+    like, any_spec, vmem_spec = jax.ShapeDtypeStruct, pl.BlockSpec(memory_space=ANY), pl.BlockSpec(memory_space=VMEM)
+    operands = (*arrays, *weights)
     return pl.pallas_call(
-        functools.partial(sum_kernel, n, arrays),
-        out_shape=(jax.ShapeDtypeStruct((count, r, ff), BF16), jax.ShapeDtypeStruct((8, 128), F32)),
-        in_specs=[pl.BlockSpec(memory_space=ANY)] * len(arrays),
-        out_specs=(pl.BlockSpec(memory_space=VMEM), pl.BlockSpec(memory_space=VMEM)),
+        functools.partial(sum_kernel, n, len(operands)),
+        out_shape=(like((count, r, ff), BF16), like((8, 128), F32), like((tokens, ff), BF16), like((tokens, ff), BF16)),
+        in_specs=[any_spec] * len(operands),
+        out_specs=(vmem_spec, vmem_spec, any_spec, any_spec),
         scratch_shapes=[
             VMEM((2, tokens, d), BF16),
             VMEM((2, tokens, d), BF16),
+            VMEM((d, width), BF16),
+            VMEM((d, width), BF16),
+            VMEM((width, d), BF16),
             VMEM((6, chips, r, ff), BF16),
             VMEM((count, chips, r, ff), BF16),
             VMEM((count, 2, chips, r, ff // 2), BF16),
             VMEM((r, ff // 2), F32),
             VMEM((n, 8, 128), F32),
             dma((2, 2)),
+            dma((7,)),
             dma((count,)),
             dma((count,)),
             dma((count, 2, chips - 1)),
@@ -216,7 +305,7 @@
         ],
         compiler_params=pltpu.CompilerParams(collective_id=0, has_side_effects=True, vmem_limit_bytes=VMEM_BYTES),
         name="gradient_sum",
-    )(*arrays)
+    )(*operands)
 
 
 WEIGHTS = ((2, 1), (0, 1), (1, 1), (2, 0), (0, 0), (1, 0))
@@ -345,7 +434,7 @@
     m, v = ([t.reshape(s) for t, s in zip(ts, row, strict=True)] for ts in (m, v))
     held = pl.pallas_call(
         functools.partial(gather_kernel, n),
-        out_shape=(*[VMEM((n, r, ff), BF16)] * count, VMEM((count, r, ff), F32), VMEM((count, r, ff), F32)),
+        out_shape=(*[VMEM((n, r, ff), BF16)] * count, *[jax.ShapeDtypeStruct((count, r, ff), F32)] * 2),
         in_specs=[vmem_spec] * 2 + [any_spec] * 9,
         out_specs=(any_spec,) * (count + 2),
         scratch_shapes=[
@@ -414,7 +503,7 @@
     return lax.dot_general(a, b, (((1,), (1,)), ((), ())), preferred_element_type=F32)
 
 
-def forward_kernel(chunks, x_ref, wg_ref, wu_ref, wd_ref, a_ref, hid_ref, gate_ref, up_ref, h_ref, acc):
+def forward_kernel(chunks, x_ref, wg_ref, wu_ref, wd_ref, a_ref, hid_ref, h_ref, acc):
     i = pl.program_id(0)
     size = x_ref.shape[0] // chunks
 
@@ -426,7 +515,7 @@
         rows = slice(q * size, (q + 1) * size)
         gate, up = dot(a_ref[rows], wg_ref[...]), dot(a_ref[rows], wu_ref[...])
         hid = (gate * jax.nn.sigmoid(gate) * up).astype(BF16)
-        gate_ref[rows], up_ref[rows], hid_ref[rows] = gate, up, hid
+        hid_ref[rows] = hid
         more = dot(hid, wd_ref[...])
 
         @pl.when(i == 0)
@@ -469,21 +558,13 @@
         dh_ref[...] = dy_ref[...] + back_through_norm(h_ref[...], da)
 
 
-def back_kernel(chunks, dy_ref, gate_ref, up_ref, wd_ref, dgate_ref, dup_ref):
-    size = dy_ref.shape[0] // chunks
-    for q in range(chunks):
-        rows = slice(q * size, (q + 1) * size)
-        gate = gate_ref[rows]
-        dgate_ref[rows], dup_ref[rows] = back_through_product(gate, up_ref[rows], jax.nn.sigmoid(gate), dot_t(dy_ref[rows], wd_ref[...]))
-
-
 def operands(x, dy, w_gate, w_up, w_down):
     (tokens, d), ff = x.shape, w_gate.shape[2]
     tile, chunks = ff // 6, 4
     grid = (ff // tile,)
     like = jax.ShapeDtypeStruct
     state, states = pl.BlockSpec((tokens, d), lambda i: (0, 0)), like((tokens, d), BF16)
-    hidden, hiddens, wide = pl.BlockSpec((tokens, tile), lambda i: (0, i)), like((tokens, ff), BF16), like((tokens, ff), F32)
+    hidden, hiddens = pl.BlockSpec((tokens, tile), lambda i: (0, i)), like((tokens, ff), BF16)
 
     def into(layer):
         return pl.BlockSpec((None, d, tile), lambda i: (layer, 0, i))
@@ -493,12 +574,12 @@
 
     acc = VMEM((tokens, d), F32)
     params = pltpu.CompilerParams(vmem_limit_bytes=56 * 1024 * 1024, dimension_semantics=("arbitrary",))
-    a0, hid0, gate0, up0, h1 = pl.pallas_call(
+    a0, hid0, h1 = pl.pallas_call(
         functools.partial(forward_kernel, chunks),
         grid=grid,
-        out_shape=(states, hiddens, wide, wide, states),
+        out_shape=(states, hiddens, states),
         in_specs=[state, into(0), into(0), out_of(0)],
-        out_specs=(state, hidden, hidden, hidden, state),
+        out_specs=(state, hidden, state),
         scratch_shapes=[acc],
         compiler_params=params,
         name="first_forward",
@@ -513,16 +594,7 @@
         compiler_params=params,
         name="last_layer",
     )(h1, dy, w_gate, w_up, w_down)
-    dgate0, dup0 = pl.pallas_call(
-        functools.partial(back_kernel, chunks),
-        grid=grid,
-        out_shape=(hiddens, hiddens),
-        in_specs=[state, hidden, hidden, out_of(0)],
-        out_specs=(hidden, hidden),
-        compiler_params=params,
-        name="first_back",
-    )(dy0, gate0, up0, w_down)
-    return hid1, a1, dgate1, dup1, dy, hid0, a0, dgate0, dup0, dy0
+    return hid1, a1, dgate1, dup1, dy, hid0, a0, dy0
 
 
 def solution(mesh):
@@ -530,7 +602,7 @@
 
     def device(x, dy, *arrays):
         w, m, v = (arrays[i : i + 3] for i in (0, 3, 6))
-        g, total = summed(n, operands(x[0], dy[0], *w))
+        g, total, *_ = summed(n, operands(x[0], dy[0], *w), w)
         return tuple(stepped(n, g, total, w, m, v))
 
     whole, rows = P(None, None, None), P(None, "dp", None)

time: 422 us -> 409 us (0.969)
  Pallas kernels: 411 us -> 395 us
    pallas_call x2 -> x1, Pallas kernels: 187 us -> 171 us  [summed(): pl.pallas_call(functools.partial(sum_kernel, n, len(operands)), out_shape...]
    unnamed x10 -> x18, local copies, waits for them, and re-layouts: 9.72 us -> 12.3 us
where the time goes in v2:
time: 409 us; the launch traced here: 408 us
  Pallas kernels  395 us (97%)
  local copies, waits for them, and re-layouts  12.3 us (3%)
    pallas_call x1, Pallas kernels, summed(): pl.pallas_call(functools.partial(sum_kernel, n, len(operands)), out_shape...  171 us
    pallas_call x1, Pallas kernels, stepped(): pl.pallas_call(functools.partial(gather_kernel, n), out_shape=(*[VMEM((n,...  146 us
    pallas_call x1, Pallas kernels, operands(): pl.pallas_call(functools.partial(turn_kernel, chunks), grid=grid, out_sha...  37.2 us
    pallas_call x1, Pallas kernels, operands(): pl.pallas_call(functools.partial(forward_kernel, chunks), grid=grid, out_...  29.2 us
    unnamed x18, local copies, waits for them, and re-layouts  12.3 us
    pallas_call x1, Pallas kernels, stepped(): pl.pallas_call(write_out, out_shape=tuple((jax.ShapeDtypeStruct(t.shape,...  12.1 us

profile of v2, /device:TPU:21, one launch (start us, length us, event | category | flops | bytes accessed | tf_op | source)
XLA Modules:
  0.0 408.1 jit_solution(13002794518403526493)
XLA Ops:
  0.6 29.2 %first_forward.1 = (bf16[1024,768]{1,0:T(8,128)(2,1)}, bf16[1024,3072]{1,0:T(8,128)(2,1)}, bf16[1024,768]{1,0:T(8,128)(2,1)}) custom-call(bf16[1024,768]{1,0:T(8,128)(2,1)} %bitcast.19, bf16[2,768,3072]{2,1,0:T(8,128)(2,1)} %refs_8_.1, bf16[2,768,3072]{2,1,0:T(8,128)(2,1)} %refs_9_.1, bf16[2,3072,768]{2,1,0:T(8,128)(2,1)} %refs_10_.1), custom_call_target="tpu_custom_call" | custom-call | tf_op jit(solution)/shard_map/first_forward/pallas_call | solution.py:577
  29.8 37.2 %last_layer.1 = (bf16[1024,768]{1,0:T(8,128)(2,1)}, bf16[1024,3072]{1,0:T(8,128)(2,1)}, bf16[1024,3072]{1,0:T(8,128)(2,1)}, bf16[1024,3072]{1,0:T(8,128)(2,1)}, bf16[1024,768]{1,0:T(8,128)(2,1)}) custom-call(bf16[1024,768]{1,0:T(8,128)(2,1)} %get-tuple-element.36.h_ref, bf16[1024,768]{1,0:T(8,128)(2,1)} %bitcast.17, bf16[2,768,3072]{2,1,0:T(8,128)(2,1)} %refs_8_.1, ...), custom_call_target="tpu_custom_call" | custom-call | tf_op jit(solution)/shard_map/last_layer/pallas_call | solution.py:587
  67.1 170.8 %gradient_sum.1 = (bf16[6,48,3072]{2,1,0:T(8,128)(2,1)}, f32[8,128]{1,0:T(8,128)}, bf16[1024,3072]{1,0:T(8,128)(2,1)}, bf16[1024,3072]{1,0:T(8,128)(2,1)}) custom-call(bf16[1024,3072]{1,0:T(8,128)(2,1)} %get-tuple-element.37.refs_0_, bf16[1024,768]{1,0:T(8,128)(2,1)} %get-tuple-element.38.refs_1_, bf16[1024,3072]{1,0:T(8,128)(2,1)} %get-tuple-element.39.refs_2_, ...), custom_call_target="tpu_custom_call" | custom-call | tf_op jit(solution)/shard_map/gradient_sum/pallas_call | solution.py:281
  237.9 0.0 copy-start.2
  237.9 1.3 copy-done.2
  239.2 0.0 copy-start.3
  239.2 1.3 copy-done.3
  240.4 0.0 copy-start.4
  240.4 1.3 copy-done.4
  241.7 0.0 copy-start.5
  241.7 1.3 copy-done.5
  243.0 0.0 copy-start.6
  243.0 1.3 copy-done.6
  244.2 0.0 copy-start.7
  244.2 1.3 copy-done.7
  245.5 0.0 copy-start.8
  245.5 0.7 copy-done.8
  246.2 145.7 %step_and_gather.1 = (bf16[16,48,3072]{2,1,0:T(8,128)(2,1)S(1)}, bf16[16,48,3072]{2,1,0:T(8,128)(2,1)S(1)}, bf16[16,48,3072]{2,1,0:T(8,128)(2,1)S(1)}, bf16[16,4...) custom-call(bf16[6,48,3072]{2,1,0:T(8,128)(2,1)} %get-tuple-element., ...), custom_call_target="tpu_custom_call" | custom-call | tf_op jit(solution)/shard_map/step_and_gather/pallas_call | solution.py:435
  391.9 0.0 copy-start
  391.9 2.0 copy-done
  393.9 0.0 copy-start.1
  393.9 2.0 copy-done.1
  395.9 12.1 %write_out.1 = (bf16[2,16,48,3072]{3,2,1,0:T(8,128)(2,1)}, bf16[2,16,48,3072]{3,2,1,0:T(8,128)(2,1)}, bf16[2,16,4,48,768]{4,3,2,1,0:T(8,128)(2,1)}, f32[2,48,307...) custom-call(bf16[16,48,3072]{2,1,0:T(8,128)(2,1)S(1)} %get-tuple-ele, ...), custom_call_target="tpu_custom_call" | custom-call | tf_op jit(solution)/shard_map/write_out/pallas_call | solution.py:465
Async XLA Ops:
  237.9 1.3 copy-start.2
  239.2 1.3 copy-start.3
  240.4 1.3 copy-start.4
  241.7 1.3 copy-start.5
  243.0 1.3 copy-start.6
  244.2 1.3 copy-start.7
  245.5 0.7 copy-start.8
  391.9 2.0 copy-start
  393.9 2.0 copy-start.1

commit v3 on v2

--- a/solution.py
+++ b/solution.py
@@ -8,7 +8,7 @@
 from jax.sharding import PartitionSpec as P
 
 F32, BF16 = jnp.float32, jnp.bfloat16
-ANY, VMEM = pl.ANY, pltpu.VMEM
+ANY, HBM, VMEM = pl.ANY, pltpu.HBM, pltpu.VMEM
 MESH = pl.DeviceIdType.MESH
 VMEM_BYTES = 64 * 1024 * 1024 - 65536
 
@@ -20,10 +20,12 @@
 
 
 def enter(peers):
-    barrier = pltpu.get_barrier_semaphore()
     for peer in peers:
-        pl.semaphore_signal(barrier, inc=1, device_id={"dp": peer}, device_id_type=MESH)
-    pl.semaphore_wait(barrier, len(peers))
+        pl.semaphore_signal(pltpu.get_barrier_semaphore(), inc=1, device_id={"dp": peer}, device_id_type=MESH)
+
+
+def meet(count):
+    pl.semaphore_wait(pltpu.get_barrier_semaphore(), count)
 
 
 def sum_kernel(n, inputs_count, *refs):
@@ -127,7 +129,7 @@
     def hop(k, way, s):
         return remote(ring.at[k, way, s], ring.at[k, way, s + 1], ring_send.at[k, way, s], ring_recv.at[k, way, s], onward[way])
 
-    def tile(index):
+    def tile(index, swaps=True):
         k, t, slot = lax.div(index, tiles), lax.rem(index, tiles), lax.rem(index, 2)
 
         @pl.when(jnp.logical_and(index + 1 < count * tiles, index + 1 != 4 * tiles))
@@ -159,9 +161,11 @@
                 buf = same * lax.rem(k, 4) + (1 - same) * (4 + lax.rem(k, 2))
                 mine[buf, lax.div(device, 2), :, pl.ds(pl.multiple_of(at, d), d)] = out[i * r : (i + 1) * r]
 
-        @pl.when(t == tiles - 1)
-        def _():
-            swap(k).start()
+        if swaps:
+
+            @pl.when(t == tiles - 1)
+            def _():
+                swap(k).start()
 
     def term(k, way, chip):
         cols = slice(way * half, (way + 1) * half)
@@ -189,9 +193,16 @@
             g_ref[k, :, way * half : (way + 1) * half] = g
             squares[...] += g.astype(F32) * g.astype(F32)
 
+    enter([lax.rem(me + o, n) for o in range(1, n)])
     start_load(0)
     squares[...] = jnp.zeros_like(squares)
-    enter([lax.rem(me + o, n) for o in range(1, n)])
+
+    @pl.loop(0, tiles)
+    def _(index):
+        tile(index, swaps=False)
+
+    meet(n - 1)
+    swap(jnp.int32(0)).start()
 
     @pl.loop(0, pairs + 1)
     def _(ii):
@@ -214,7 +225,7 @@
 
                 place = 2 * s + j - shift * lax.div(ii, 2)
 
-                @pl.when(jnp.logical_and(ii < pairs, jnp.logical_and(place >= 0, place < 2 * tiles)))
+                @pl.when(jnp.logical_and(ii < pairs, jnp.logical_and(place >= tiles * (1 - lax.div(ii + 2, 3)), place < 2 * tiles)))
                 def _():
                     tile(2 * tiles * ii + place)
 
@@ -367,10 +378,10 @@
         ref = part(k, way, s)
         return remote(ref if source is None else source, ref, pair_send.at[k, way, s], pair_recv.at[k, way, s], partner)
 
+    enter((partner, left, right))
     for k in range(count):
         for copy in loads(k):
             copy.start()
-    enter((partner, left, right))
     factor = jnp.minimum(1.0, 0.5 * lax.rsqrt(total_ref[0:1, 0:1] * (1.0 / (count * r * ff * n)) + 1e-30))
 
     for k in range(count):
@@ -389,6 +400,8 @@
             v_buf[k, :, cols] = v
             w_buf[k, :, cols] = (w - 0.02 * step).astype(BF16)
 
+        if k == 0:
+            meet(3)
         for way in range(2):
             own = w_buf.at[k, :, pl.ds(way * half, half)]
             hop(k, way, 0, own).start()
@@ -432,6 +445,7 @@
     whole = (layers, n, r, ff), (layers, n, r, ff), (layers, n, tiles, r, d)
     w = [t.reshape(s) for t, s in zip(w, whole, strict=True)]
     m, v = ([t.reshape(s) for t, s in zip(ts, row, strict=True)] for ts in (m, v))
+    m, v = ([pltpu.with_memory_space_constraint(t, HBM) for t in ts] for ts in (m, v))
     held = pl.pallas_call(
         functools.partial(gather_kernel, n),
         out_shape=(*[VMEM((n, r, ff), BF16)] * count, *[jax.ShapeDtypeStruct((count, r, ff), F32)] * 2),
@@ -444,7 +458,7 @@
             *[dma((count, 2, chips - 1)) for _ in range(2)],
             *[dma((count, 2, chips)) for _ in range(2)],
         ],
-        compiler_params=pltpu.CompilerParams(collective_id=1, has_side_effects=True, vmem_limit_bytes=20 * 1024 * 1024),
+        compiler_params=pltpu.CompilerParams(collective_id=1, has_side_effects=True, vmem_limit_bytes=27 * 1024 * 1024),
         name="step_and_gather",
     )(g, total, *w, *m, *v)
 
@@ -510,21 +524,14 @@
     @pl.when(i == 0)
     def _():
         a_ref[...] = normed(x_ref[...])
+        acc[...] = jnp.zeros_like(acc)
 
     for q in range(chunks):
         rows = slice(q * size, (q + 1) * size)
         gate, up = dot(a_ref[rows], wg_ref[...]), dot(a_ref[rows], wu_ref[...])
         hid = (gate * jax.nn.sigmoid(gate) * up).astype(BF16)
         hid_ref[rows] = hid
-        more = dot(hid, wd_ref[...])
-
-        @pl.when(i == 0)
-        def _():
-            acc[rows] = more
-
-        @pl.when(i > 0)
-        def _():
-            acc[rows] += more
+        acc[rows] += dot(hid, wd_ref[...])
 
     @pl.when(i == pl.num_programs(0) - 1)
     def _():
@@ -560,7 +567,7 @@
 
 def operands(x, dy, w_gate, w_up, w_down):
     (tokens, d), ff = x.shape, w_gate.shape[2]
-    tile, chunks = ff // 6, 4
+    tile, chunks = ff // 6, 2
     grid = (ff // tile,)
     like = jax.ShapeDtypeStruct
     state, states = pl.BlockSpec((tokens, d), lambda i: (0, 0)), like((tokens, d), BF16)

time: 409 us -> 389 us (0.951)
  Pallas kernels: 395 us -> 384 us
  local copies, waits for them, and re-layouts: 12.3 us -> 3.99 us
    unnamed x18 -> x4, local copies, waits for them, and re-layouts: 12.3 us -> 3.99 us
    pallas_call x1, Pallas kernels: 29.2 us -> 22 us  [operands(): pl.pallas_call(functools.partial(forward_kernel, chunks), grid=grid, out_...]
where the time goes in v3:
time: 389 us; the launch traced here: 388 us
  Pallas kernels  384 us (99%)
  local copies, waits for them, and re-layouts  3.99 us (1%)
    pallas_call x1, Pallas kernels, summed(): pl.pallas_call(functools.partial(sum_kernel, n, len(operands)), out_shape...  170 us
    pallas_call x1, Pallas kernels, stepped(): pl.pallas_call(functools.partial(gather_kernel, n), out_shape=(*[VMEM((n,...  144 us
    pallas_call x1, Pallas kernels, operands(): pl.pallas_call(functools.partial(turn_kernel, chunks), grid=grid, out_sha...  35.4 us
    pallas_call x1, Pallas kernels, operands(): pl.pallas_call(functools.partial(forward_kernel, chunks), grid=grid, out_...  22 us
    pallas_call x1, Pallas kernels, stepped(): pl.pallas_call(write_out, out_shape=tuple((jax.ShapeDtypeStruct(t.shape,...  12.1 us

profile of v3, /device:TPU:21, one launch (start us, length us, event | category | flops | bytes accessed | tf_op | source)
XLA Modules:
  0.0 388.4 jit_solution(2043431028433827398)
XLA Ops:
  0.6 22.0 %first_forward.1 = (bf16[1024,768]{1,0:T(8,128)(2,1)}, bf16[1024,3072]{1,0:T(8,128)(2,1)}, bf16[1024,768]{1,0:T(8,128)(2,1)}) custom-call(bf16[1024,768]{1,0:T(8,128)(2,1)} %bitcast.17, bf16[2,768,3072]{2,1,0:T(8,128)(2,1)} %refs_8_.1, bf16[2,768,3072]{2,1,0:T(8,128)(2,1)} %refs_9_.1, bf16[2,3072,768]{2,1,0:T(8,128)(2,1)} %refs_10_.1), custom_call_target="tpu_custom_call" | custom-call | tf_op jit(solution)/shard_map/first_forward/pallas_call | solution.py:584
  22.6 35.4 %last_layer.1 = (bf16[1024,768]{1,0:T(8,128)(2,1)}, bf16[1024,3072]{1,0:T(8,128)(2,1)}, bf16[1024,3072]{1,0:T(8,128)(2,1)}, bf16[1024,3072]{1,0:T(8,128)(2,1)}, bf16[1024,768]{1,0:T(8,128)(2,1)}) custom-call(bf16[1024,768]{1,0:T(8,128)(2,1)} %get-tuple-element.36.h_ref, bf16[1024,768]{1,0:T(8,128)(2,1)} %bitcast.15, bf16[2,768,3072]{2,1,0:T(8,128)(2,1)} %refs_8_.1, ...), custom_call_target="tpu_custom_call" | custom-call | tf_op jit(solution)/shard_map/last_layer/pallas_call | solution.py:594
  58.1 170.4 %gradient_sum.1 = (bf16[6,48,3072]{2,1,0:T(8,128)(2,1)}, f32[8,128]{1,0:T(8,128)}, bf16[1024,3072]{1,0:T(8,128)(2,1)}, bf16[1024,3072]{1,0:T(8,128)(2,1)}) custom-call(bf16[1024,3072]{1,0:T(8,128)(2,1)} %get-tuple-element.37.refs_0_, bf16[1024,768]{1,0:T(8,128)(2,1)} %get-tuple-element.38.refs_1_, bf16[1024,3072]{1,0:T(8,128)(2,1)} %get-tuple-element.39.refs_2_, ...), custom_call_target="tpu_custom_call" | custom-call | tf_op jit(solution)/shard_map/gradient_sum/pallas_call | solution.py:292
  228.5 143.7 %step_and_gather.1 = (bf16[16,48,3072]{2,1,0:T(8,128)(2,1)S(1)}, bf16[16,48,3072]{2,1,0:T(8,128)(2,1)S(1)}, bf16[16,48,3072]{2,1,0:T(8,128)(2,1)S(1)}, bf16[16,4...) custom-call(bf16[6,48,3072]{2,1,0:T(8,128)(2,1)} %get-tuple-element., ...), custom_call_target="tpu_custom_call" | custom-call | tf_op jit(solution)/shard_map/step_and_gather/pallas_call | solution.py:449
  372.2 0.0 copy-start
  372.2 2.0 copy-done
  374.2 0.0 copy-start.1
  374.2 2.0 copy-done.1
  376.2 12.1 %write_out.1 = (bf16[2,16,48,3072]{3,2,1,0:T(8,128)(2,1)}, bf16[2,16,48,3072]{3,2,1,0:T(8,128)(2,1)}, bf16[2,16,4,48,768]{4,3,2,1,0:T(8,128)(2,1)}, f32[2,48,307...) custom-call(bf16[16,48,3072]{2,1,0:T(8,128)(2,1)S(1)} %get-tuple-ele, ...), custom_call_target="tpu_custom_call" | custom-call | tf_op jit(solution)/shard_map/write_out/pallas_call | solution.py:479
Async XLA Ops:
  372.2 2.0 copy-start
  374.2 2.0 copy-start.1

commit v4 on v3

--- a/solution.py
+++ b/solution.py
@@ -29,11 +29,11 @@
 
 
 def sum_kernel(n, inputs_count, *refs):
-    *inputs, wg, wu, wd = refs[:inputs_count]
+    hid, a, dgate1, dup1, dy, dh, wg, wu, wd = refs[:inputs_count]
     g_ref, total_ref, dgate, dup = refs[inputs_count : inputs_count + 4]
     (a_buf, b_buf, wg_buf, wu_buf, wd_buf, mine, theirs, ring, squares, slots, *sems) = refs[inputs_count + 4 :]
     load_sem, back_sem, swap_send, swap_recv, ring_send, ring_recv, all_send, all_recv = sems
-    inputs += [dgate, dup]
+    inputs = [hid.at[1], a.at[1], dgate1, dup1, dy, hid.at[0], a.at[0], dh, dgate, dup]
     d = a_buf.shape[2]
     r, ff = mine.shape[2:]
     half, tiles, chips = ff // 2, ff // d, n // 2
@@ -211,7 +211,7 @@
             for j in range(2):
                 k = 2 * (ii - 1) + j
 
-                @pl.when(jnp.logical_and(ii > 0, s == 0))
+                @pl.when(jnp.logical_and(ii > 0, jnp.logical_and(s == 0, k > 0)))
                 def _():
                     first(k)
 
@@ -222,6 +222,12 @@
                 @pl.when(jnp.logical_and(ii > 1, s == 0))
                 def _():
                     last(k - 2)
+
+                if j == 0:
+
+                    @pl.when(jnp.logical_and(ii == 0, s == tiles - 1))
+                    def _():
+                        first(jnp.int32(0))
 
                 place = 2 * s + j - shift * lax.div(ii, 2)
 
@@ -283,8 +289,8 @@
 
 
 def summed(n, arrays, weights):
-    tokens, d = arrays[1].shape
-    ff = arrays[0].shape[1]
+    tokens, d = arrays[1].shape[1:]
+    ff = arrays[0].shape[2]
     r, chips, count, width = d // n, n // 2, len(SOURCES), ff // 6
     dma = pltpu.SemaphoreType.DMA
     like, any_spec, vmem_spec = jax.ShapeDtypeStruct, pl.BlockSpec(memory_space=ANY), pl.BlockSpec(memory_space=VMEM)
@@ -517,91 +523,84 @@
     return lax.dot_general(a, b, (((1,), (1,)), ((), ())), preferred_element_type=F32)
 
 
-def forward_kernel(chunks, x_ref, wg_ref, wu_ref, wd_ref, a_ref, hid_ref, h_ref, acc):
-    i = pl.program_id(0)
+def layers_kernel(chunks, x_ref, dy_ref, wg_ref, wu_ref, wd_ref, a_ref, hid_ref, dgate_ref, dup_ref, dh_ref, h, acc_g, acc_u):
+    turn, i, end = pl.program_id(0) == 1, pl.program_id(1), pl.num_programs(1) - 1
+    first = jnp.logical_not(turn)
     size = x_ref.shape[0] // chunks
 
-    @pl.when(i == 0)
+    @pl.when(jnp.logical_and(first, i == 0))
     def _():
         a_ref[...] = normed(x_ref[...])
-        acc[...] = jnp.zeros_like(acc)
-
-    for q in range(chunks):
-        rows = slice(q * size, (q + 1) * size)
-        gate, up = dot(a_ref[rows], wg_ref[...]), dot(a_ref[rows], wu_ref[...])
-        hid = (gate * jax.nn.sigmoid(gate) * up).astype(BF16)
-        hid_ref[rows] = hid
-        acc[rows] += dot(hid, wd_ref[...])
-
-    @pl.when(i == pl.num_programs(0) - 1)
+        acc_g[...] = jnp.zeros_like(acc_g)
+
+    @pl.when(jnp.logical_and(turn, i == 0))
     def _():
-        h_ref[...] = x_ref[...] + acc[...].astype(BF16)
-
-
-def turn_kernel(chunks, h_ref, dy_ref, wg_ref, wu_ref, wd_ref, a_ref, hid_ref, dgate_ref, dup_ref, dh_ref, acc_g, acc_u):
-    i = pl.program_id(0)
-    size = h_ref.shape[0] // chunks
-
-    @pl.when(i == 0)
-    def _():
-        a_ref[...] = normed(h_ref[...])
+        a_ref[...] = normed(h[...])
         acc_g[...] = jnp.zeros_like(acc_g)
         acc_u[...] = jnp.zeros_like(acc_u)
 
-    for q in range(chunks):
-        rows = slice(q * size, (q + 1) * size)
-        gate, up = dot(a_ref[rows], wg_ref[...]), dot(a_ref[rows], wu_ref[...])
-        dhid = dot_t(dy_ref[rows], wd_ref[...])
-        s = jax.nn.sigmoid(gate)
-        hid_ref[rows] = (gate * s * up).astype(BF16)
-        dgate, dup = back_through_product(gate, up, s, dhid)
-        dgate_ref[rows], dup_ref[rows] = dgate, dup
-        acc_g[rows] += dot_t(dgate, wg_ref[...])
-        acc_u[rows] += dot_t(dup, wu_ref[...])
-
-    @pl.when(i == pl.num_programs(0) - 1)
+    @pl.when(first)
+    def _():
+        for q in range(chunks):
+            rows = slice(q * size, (q + 1) * size)
+            gate, up = dot(a_ref[rows], wg_ref[...]), dot(a_ref[rows], wu_ref[...])
+            hid = (gate * jax.nn.sigmoid(gate) * up).astype(BF16)
+            hid_ref[rows] = hid
+            acc_g[rows] += dot(hid, wd_ref[...])
+
+    @pl.when(turn)
+    def _():
+        for q in range(chunks):
+            rows = slice(q * size, (q + 1) * size)
+            gate, up = dot(a_ref[rows], wg_ref[...]), dot(a_ref[rows], wu_ref[...])
+            dhid = dot_t(dy_ref[rows], wd_ref[...])
+            s = jax.nn.sigmoid(gate)
+            hid_ref[rows] = (gate * s * up).astype(BF16)
+            dgate, dup = back_through_product(gate, up, s, dhid)
+            dgate_ref[rows], dup_ref[rows] = dgate, dup
+            acc_g[rows] += dot_t(dgate, wg_ref[...])
+            acc_u[rows] += dot_t(dup, wu_ref[...])
+
+    @pl.when(jnp.logical_and(first, i == end))
+    def _():
+        h[...] = x_ref[...] + acc_g[...].astype(BF16)
+
+    @pl.when(jnp.logical_and(turn, i == end))
     def _():
         da = acc_g[...].astype(BF16) + acc_u[...].astype(BF16)
-        dh_ref[...] = dy_ref[...] + back_through_norm(h_ref[...], da)
+        dh_ref[...] = dy_ref[...] + back_through_norm(h[...], da)
 
 
 def operands(x, dy, w_gate, w_up, w_down):
-    (tokens, d), ff = x.shape, w_gate.shape[2]
+    (tokens, d), (layers, _, ff) = x.shape, w_gate.shape
     tile, chunks = ff // 6, 2
-    grid = (ff // tile,)
     like = jax.ShapeDtypeStruct
-    state, states = pl.BlockSpec((tokens, d), lambda i: (0, 0)), like((tokens, d), BF16)
-    hidden, hiddens = pl.BlockSpec((tokens, tile), lambda i: (0, i)), like((tokens, ff), BF16)
-
-    def into(layer):
-        return pl.BlockSpec((None, d, tile), lambda i: (layer, 0, i))
-
-    def out_of(layer):
-        return pl.BlockSpec((None, tile, d), lambda i: (layer, i, 0))
-
-    acc = VMEM((tokens, d), F32)
-    params = pltpu.CompilerParams(vmem_limit_bytes=56 * 1024 * 1024, dimension_semantics=("arbitrary",))
-    a0, hid0, h1 = pl.pallas_call(
-        functools.partial(forward_kernel, chunks),
-        grid=grid,
-        out_shape=(states, hiddens, states),
-        in_specs=[state, into(0), into(0), out_of(0)],
-        out_specs=(state, hidden, state),
-        scratch_shapes=[acc],
-        compiler_params=params,
-        name="first_forward",
-    )(x, w_gate, w_up, w_down)
-    a1, hid1, dgate1, dup1, dy0 = pl.pallas_call(
-        functools.partial(turn_kernel, chunks),
-        grid=grid,
-        out_shape=(states, hiddens, hiddens, hiddens, states),
-        in_specs=[state, state, into(1), into(1), out_of(1)],
-        out_specs=(state, hidden, hidden, hidden, state),
-        scratch_shapes=[acc, acc],
-        compiler_params=params,
-        name="last_layer",
-    )(h1, dy, w_gate, w_up, w_down)
-    return hid1, a1, dgate1, dup1, dy, hid0, a0, dy0
+    state = pl.BlockSpec((tokens, d), lambda l, i: (0, 0))
+    into = pl.BlockSpec((None, d, tile), lambda l, i: (l, 0, i))
+    last = pl.BlockSpec((tokens, tile), lambda l, i: (0, l * i))
+    a, hid, dgate, dup, dh = pl.pallas_call(
+        functools.partial(layers_kernel, chunks),
+        grid=(layers, ff // tile),
+        out_shape=(
+            like((layers, tokens, d), BF16),
+            like((layers, tokens, ff), BF16),
+            like((tokens, ff), BF16),
+            like((tokens, ff), BF16),
+            like((tokens, d), BF16),
+        ),
+        in_specs=[state, state, into, into, pl.BlockSpec((None, tile, d), lambda l, i: (l, i, 0))],
+        out_specs=(
+            pl.BlockSpec((None, tokens, d), lambda l, i: (l, 0, 0)),
+            pl.BlockSpec((None, tokens, tile), lambda l, i: (l, 0, i)),
+            last,
+            last,
+            state,
+        ),
+        scratch_shapes=[VMEM((tokens, d), BF16), VMEM((tokens, d), F32), VMEM((tokens, d), F32)],
+        compiler_params=pltpu.CompilerParams(vmem_limit_bytes=58 * 1024 * 1024, dimension_semantics=("arbitrary", "arbitrary")),
+        name="layers",
+    )(x, dy, w_gate, w_up, w_down)
+    return hid, a, dgate, dup, dy, dh
 
 
 def solution(mesh):

time: 389 us -> 386 us (level)
    pallas_call x2 -> x1, Pallas kernels: 57.4 us -> 54.1 us  [operands(): pl.pallas_call(functools.partial(layers_kernel, chunks), grid=(layers, ff...]
where the time goes in v4:
time: 386 us
  Pallas kernels  381 us (99%)
  local copies, waits for them, and re-layouts  3.99 us (1%)
    pallas_call x1, Pallas kernels, summed(): pl.pallas_call(functools.partial(sum_kernel, n, len(operands)), out_shape...  170 us
    pallas_call x1, Pallas kernels, stepped(): pl.pallas_call(functools.partial(gather_kernel, n), out_shape=(*[VMEM((n,...  144 us
    pallas_call x1, Pallas kernels, operands(): pl.pallas_call(functools.partial(layers_kernel, chunks), grid=(layers, ff...  54.1 us
    pallas_call x1, Pallas kernels, stepped(): pl.pallas_call(write_out, out_shape=tuple((jax.ShapeDtypeStruct(t.shape,...  12.1 us

profile of v4, /device:TPU:21, one launch (start us, length us, event | category | flops | bytes accessed | tf_op | source)
XLA Modules:
  0.0 385.5 jit_solution(13418390173039297533)
XLA Ops:
  0.6 54.1 %layers.1 = (bf16[2,1024,768]{2,1,0:T(8,128)(2,1)}, bf16[2,1024,3072]{2,1,0:T(8,128)(2,1)}, bf16[1024,3072]{1,0:T(8,128)(2,1)}, bf16[1024,3072]{1,0:T(8,128)(2,1)}, bf16[1024,768]{1,0:T(8,128)(2,1)}) custom-call(bf16[1024,768]{1,0:T(8,128)(2,1)} %bitcast.17, bf16[1024,768]{1,0:T(8,128)(2,1)} %bitcast.15, bf16[2,768,3072]{2,1,0:T(8,128)(2,1)} %refs_6_.2, ...), custom_call_target="tpu_custom_call" | custom-call | tf_op jit(solution)/shard_map/layers/pallas_call | solution.py:581
  54.7 170.2 %gradient_sum.1 = (bf16[6,48,3072]{2,1,0:T(8,128)(2,1)}, f32[8,128]{1,0:T(8,128)}, bf16[1024,3072]{1,0:T(8,128)(2,1)}, bf16[1024,3072]{1,0:T(8,128)(2,1)}) custom-call(bf16[2,1024,3072]{2,1,0:T(8,128)(2,1)} %get-tuple-element.33.refs_0_, bf16[2,1024,768]{2,1,0:T(8,128)(2,1)} %get-tuple-element.34.refs_1_, bf16[1024,3072]{1,0:T(8,128)(2,1)} %get-tuple-element.35.refs_2_, ...), custom_call_target="tpu_custom_call" | custom-call | tf_op jit(solution)/shard_map/gradient_sum/pallas_call | solution.py:298
  224.9 144.4 %step_and_gather.1 = (bf16[16,48,3072]{2,1,0:T(8,128)(2,1)S(1)}, bf16[16,48,3072]{2,1,0:T(8,128)(2,1)S(1)}, bf16[16,48,3072]{2,1,0:T(8,128)(2,1)S(1)}, bf16[16,4...) custom-call(bf16[6,48,3072]{2,1,0:T(8,128)(2,1)} %get-tuple-element., ...), custom_call_target="tpu_custom_call" | custom-call | tf_op jit(solution)/shard_map/step_and_gather/pallas_call | solution.py:455
  369.3 0.0 copy-start
  369.3 2.0 copy-done
  371.3 0.0 copy-start.1
  371.3 2.0 copy-done.1
  373.3 12.1 %write_out.1 = (bf16[2,16,48,3072]{3,2,1,0:T(8,128)(2,1)}, bf16[2,16,48,3072]{3,2,1,0:T(8,128)(2,1)}, bf16[2,16,4,48,768]{4,3,2,1,0:T(8,128)(2,1)}, f32[2,48,307...) custom-call(bf16[16,48,3072]{2,1,0:T(8,128)(2,1)S(1)} %get-tuple-ele, ...), custom_call_target="tpu_custom_call" | custom-call | tf_op jit(solution)/shard_map/write_out/pallas_call | solution.py:485
Async XLA Ops:
  369.3 2.0 copy-start
  371.3 2.0 copy-start.1

commit v5 on v4

--- a/solution.py
+++ b/solution.py
@@ -26,6 +26,9 @@
 
 def meet(count):
     pl.semaphore_wait(pltpu.get_barrier_semaphore(), count)
+
+
+LANES = (0, 2, 1, 3)
 
 
 def sum_kernel(n, inputs_count, *refs):
@@ -36,7 +39,7 @@
     inputs = [hid.at[1], a.at[1], dgate1, dup1, dy, hid.at[0], a.at[0], dh, dgate, dup]
     d = a_buf.shape[2]
     r, ff = mine.shape[2:]
-    half, tiles, chips = ff // 2, ff // d, n // 2
+    quarter, tiles, chips = ff // 4, ff // d, n // 2
     width = wg_buf.shape[1]
     backs = ff // width
     late = backs - (chips - 1 - tiles)
@@ -126,8 +129,9 @@
     def swap(k):
         return remote(mine.at[4 + lax.rem(k, 2)], theirs.at[k], swap_send.at[k], swap_recv.at[k], partner)
 
-    def hop(k, way, s):
-        return remote(ring.at[k, way, s], ring.at[k, way, s + 1], ring_send.at[k, way, s], ring_recv.at[k, way, s], onward[way])
+    def hop(k, lane, s):
+        to = onward[lane // 2]
+        return remote(ring.at[k, lane, s], ring.at[k, lane, s + 1], ring_send.at[k, lane, s], ring_recv.at[k, lane, s], to)
 
     def tile(index, swaps=True):
         k, t, slot = lax.div(index, tiles), lax.rem(index, tiles), lax.rem(index, 2)
@@ -167,30 +171,32 @@
             def _():
                 swap(k).start()
 
-    def term(k, way, chip):
-        cols = slice(way * half, (way + 1) * half)
-        return mine[lax.rem(k, 4), chip, :, cols].astype(F32) + theirs[k, chip, :, cols].astype(F32)
-
-    def meant_for(way, s):
-        return lax.rem(z + chips - 1 - s, chips) if way == 0 else lax.rem(z + 1 + s, chips)
+    def columns(lane):
+        return slice(lane * quarter, (lane + 1) * quarter)
+
+    def term(k, lane, chip):
+        return mine[lax.rem(k, 4), chip, :, columns(lane)].astype(F32) + theirs[k, chip, :, columns(lane)].astype(F32)
+
+    def meant_for(lane, s):
+        return lax.rem(z + chips - 1 - s, chips) if lane < 2 else lax.rem(z + 1 + s, chips)
 
     def first(k):
         swap(k).wait_recv()
-        for way in range(2):
-            ring[k, way, 0] = term(k, way, meant_for(way, 0)).astype(BF16)
-            hop(k, way, 0).start()
+        for lane in LANES:
+            ring[k, lane, 0] = term(k, lane, meant_for(lane, 0)).astype(BF16)
+            hop(k, lane, 0).start()
 
     def middle(k, s):
-        for way in range(2):
-            hop(k, way, s - 1).wait_recv()
-            ring[k, way, s] = (term(k, way, meant_for(way, s)) + ring[k, way, s].astype(F32)).astype(BF16)
-            hop(k, way, s).start()
+        for lane in LANES:
+            hop(k, lane, s - 1).wait_recv()
+            ring[k, lane, s] = (term(k, lane, meant_for(lane, s)) + ring[k, lane, s].astype(F32)).astype(BF16)
+            hop(k, lane, s).start()
 
     def last(k):
-        for way in range(2):
-            hop(k, way, chips - 2).wait_recv()
-            g = (term(k, way, z) + ring[k, way, chips - 1].astype(F32)).astype(BF16)
-            g_ref[k, :, way * half : (way + 1) * half] = g
+        for lane in LANES:
+            hop(k, lane, chips - 2).wait_recv()
+            g = (term(k, lane, z) + ring[k, lane, chips - 1].astype(F32)).astype(BF16)
+            g_ref[k, :, columns(lane)] = g
             squares[...] += g.astype(F32) * g.astype(F32)
 
     enter([lax.rem(me + o, n) for o in range(1, n)])
@@ -257,7 +263,7 @@
 
     whole = squares[0:8, 0:128]
     for i in range(r // 8):
-        for q in range(half // 128):
+        for q in range(quarter // 128):
             if i or q:
                 whole = whole + squares[i * 8 : (i + 1) * 8, q * 128 : (q + 1) * 128]
     slots[0] = whole
@@ -277,8 +283,8 @@
     def _(k):
         @pl.loop(0, chips - 1)
         def _(s):
-            for way in range(2):
-                hop(k, way, s).wait_send()
+            for lane in LANES:
+                hop(k, lane, s).wait_send()
 
     for j in range(2):
         swap(jnp.int32(count - 2 + j)).wait_send()
@@ -308,15 +314,15 @@
             VMEM((width, d), BF16),
             VMEM((6, chips, r, ff), BF16),
             VMEM((count, chips, r, ff), BF16),
-            VMEM((count, 2, chips, r, ff // 2), BF16),
-            VMEM((r, ff // 2), F32),
+            VMEM((count, 4, chips, r, ff // 4), BF16),
+            VMEM((r, ff // 4), F32),
             VMEM((n, 8, 128), F32),
             dma((2, 2)),
             dma((7,)),
             dma((count,)),
             dma((count,)),
-            dma((count, 2, chips - 1)),
-            dma((count, 2, chips - 1)),
+            dma((count, 4, chips - 1)),
+            dma((count, 4, chips - 1)),
             dma((n,)),
             dma((n,)),
         ],

time: 386 us -> 387 us (level)
  no operation moved by 1% of the time
where the time goes in v5:
time: 387 us
  Pallas kernels  382 us (99%)
  local copies, waits for them, and re-layouts  3.99 us (1%)
    pallas_call x1, Pallas kernels, summed(): pl.pallas_call(functools.partial(sum_kernel, n, len(operands)), out_shape...  172 us
    pallas_call x1, Pallas kernels, stepped(): pl.pallas_call(functools.partial(gather_kernel, n), out_shape=(*[VMEM((n,...  144 us
    pallas_call x1, Pallas kernels, operands(): pl.pallas_call(functools.partial(layers_kernel, chunks), grid=(layers, ff...  54.1 us
    pallas_call x1, Pallas kernels, stepped(): pl.pallas_call(write_out, out_shape=tuple((jax.ShapeDtypeStruct(t.shape,...  12.1 us

profile of v5, /device:TPU:21, one launch (start us, length us, event | category | flops | bytes accessed | tf_op | source)
XLA Modules:
  0.0 386.5 jit_solution(18325208380605688459)
XLA Ops:
  0.6 54.1 %layers.1 = (bf16[2,1024,768]{2,1,0:T(8,128)(2,1)}, bf16[2,1024,3072]{2,1,0:T(8,128)(2,1)}, bf16[1024,3072]{1,0:T(8,128)(2,1)}, bf16[1024,3072]{1,0:T(8,128)(2,1)}, bf16[1024,768]{1,0:T(8,128)(2,1)}) custom-call(bf16[1024,768]{1,0:T(8,128)(2,1)} %bitcast.17, bf16[1024,768]{1,0:T(8,128)(2,1)} %bitcast.15, bf16[2,768,3072]{2,1,0:T(8,128)(2,1)} %refs_6_.2, ...), custom_call_target="tpu_custom_call" | custom-call | tf_op jit(solution)/shard_map/layers/pallas_call | solution.py:587
  54.7 171.9 %gradient_sum.1 = (bf16[6,48,3072]{2,1,0:T(8,128)(2,1)}, f32[8,128]{1,0:T(8,128)}, bf16[1024,3072]{1,0:T(8,128)(2,1)}, bf16[1024,3072]{1,0:T(8,128)(2,1)}) custom-call(bf16[2,1024,3072]{2,1,0:T(8,128)(2,1)} %get-tuple-element.33.refs_0_, bf16[2,1024,768]{2,1,0:T(8,128)(2,1)} %get-tuple-element.34.refs_1_, bf16[1024,3072]{1,0:T(8,128)(2,1)} %get-tuple-element.35.refs_2_, ...), custom_call_target="tpu_custom_call" | custom-call | tf_op jit(solution)/shard_map/gradient_sum/pallas_call | solution.py:304
  226.6 143.7 %step_and_gather.1 = (bf16[16,48,3072]{2,1,0:T(8,128)(2,1)S(1)}, bf16[16,48,3072]{2,1,0:T(8,128)(2,1)S(1)}, bf16[16,48,3072]{2,1,0:T(8,128)(2,1)S(1)}, bf16[16,4...) custom-call(bf16[6,48,3072]{2,1,0:T(8,128)(2,1)} %get-tuple-element., ...), custom_call_target="tpu_custom_call" | custom-call | tf_op jit(solution)/shard_map/step_and_gather/pallas_call | solution.py:461
  370.3 0.0 copy-start
  370.3 2.0 copy-done
  372.3 0.0 copy-start.1
  372.3 2.0 copy-done.1
  374.3 12.1 %write_out.1 = (bf16[2,16,48,3072]{3,2,1,0:T(8,128)(2,1)}, bf16[2,16,48,3072]{3,2,1,0:T(8,128)(2,1)}, bf16[2,16,4,48,768]{4,3,2,1,0:T(8,128)(2,1)}, f32[2,48,307...) custom-call(bf16[16,48,3072]{2,1,0:T(8,128)(2,1)S(1)} %get-tuple-ele, ...), custom_call_target="tpu_custom_call" | custom-call | tf_op jit(solution)/shard_map/write_out/pallas_call | solution.py:491
Async XLA Ops:
  370.3 2.0 copy-start
  372.3 2.0 copy-start.1
